TPU v7x, 512 devices: a whole 4x4x16 slice. The times are simulated.
512 devices in a mesh: segment: 16 (over z_hi, y, core), dp: 32 (over x, z_lo).
Axes of the slice: x: 4, y: 4, z: 16 (z_hi: 2, z_lo: 8; z = z_hi * 8 + z_lo), core: 2. Of those that a mesh axis runs over, the one named last changes fastest.
Arguments:
- token_ids: int32 [4096], P('dp'), may hold values from 0 to 152063, as said below
- table: bfloat16 [19008, 28672], P('segment', 'dp'), may hold values from -6 to 6
- out_grad: bfloat16 [4096, 3584], P('dp', 'segment'), may hold values from -6 to 6
Outputs:
- embedded: bfloat16 [4096, 3584], P('dp')
- table_grad: bfloat16 [19008, 28672], P('segment', 'dp')
Inputs may be any that keep to these rules, and one draw needn't show every extreme that they name: `token_ids`: in the 128 tokens of each data group, at most 16 ids lie in one segment's slice of 9504 rows with one residue modulo 8; in every data group some segment and residue has exactly 16.
All inputs are finite; a program needn't handle non-finite values.
Results may differ from a plain program's by a relative error of at most 0.001.
Values may be sent and summed in bfloat16 or wider, within the bound.
A program may use at most 64 MiB of HBM per device.

v0:
```python
import jax
import jax.numpy as jnp
from jax import lax
from jax.sharding import PartitionSpec as P

D = 3584
PACK = 8


def copy_for_each(shard, axis):
    size = lax.axis_size(axis)
    return lax.all_to_all(
        jnp.broadcast_to(shard[None], (size, *shard.shape)), axis, 0, 0, tiled=True
    )


def joined_along(tiles, dim):
    tiles = jnp.moveaxis(tiles, 0, dim)
    shape = tiles.shape
    return tiles.reshape(*shape[:dim], shape[dim] * shape[dim + 1], *shape[dim + 2 :])


def collect(shard, axis, dim):
    tiles = copy_for_each(shard, axis)
    return joined_along(tiles, dim)


def filled_up(lines, size):
    spare = -lines.shape[0] % size
    if not spare:
        return lines
    return jnp.concatenate([lines, jnp.zeros((spare, *lines.shape[1:]), lines.dtype)])


def sum_in_two_steps(shard, axis):
    lines = shard.reshape(-1, *shard.shape[1:][-1:])
    padded = filled_up(lines, lax.axis_size(axis))
    own = lax.psum_scatter(padded, axis, scatter_dimension=0, tiled=True)
    whole = lax.all_gather(own, axis, axis=0, tiled=True)
    return whole[: len(lines)].reshape(shard.shape)


def body(token_ids, table, out_grad):
    lines = table.shape[0]
    width = table.shape[1]
    groups = lax.axis_size("dp")
    tok_rows = token_ids.shape[0]
    quarters = D // width
    slot = lax.axis_index("dp") // quarters
    first = lax.axis_index("segment") * lines * PACK
    every_id = collect(token_ids, "dp", 0)
    local = every_id - first
    in_section = (local >= 0) & (local < lines * PACK)
    owned = in_section & (local % PACK == slot)
    line_idx = jnp.clip(local // PACK, 0, lines - 1)
    whole_grad = lax.all_gather(out_grad, "segment", axis=1, tiled=True)
    capacity = tok_rows // PACK
    owned_grid = owned.reshape(groups, tok_rows)
    rank = jnp.cumsum(owned_grid.astype(jnp.int32), axis=1) - 1
    place = jnp.where(owned_grid, rank, capacity)
    group_rows = jnp.broadcast_to(jnp.arange(groups, dtype=jnp.int32)[:, None], (groups, tok_rows))
    row_of = (
        jnp.zeros((groups, capacity), jnp.int32)
        .at[group_rows, place]
        .set(line_idx.reshape(groups, tok_rows), mode="drop")
    )
    filled = jnp.zeros((groups, capacity), jnp.bool_).at[group_rows, place].set(True, mode="drop")
    fetched = jnp.take(table, row_of.reshape(-1), axis=0).reshape(groups, capacity, width)
    fetched = jnp.where(filled[:, :, None], fetched, jnp.zeros((), jnp.bfloat16))
    arrived = lax.all_to_all(fetched, "dp", split_axis=0, concat_axis=0, tiled=True)
    my_local = token_ids - first
    my_in = (my_local >= 0) & (my_local < lines * PACK)
    my_slot = my_local % PACK
    slot_hits = (my_slot[:, None] == jnp.arange(PACK, dtype=jnp.int32)[None, :]) & my_in[:, None]
    slot_ranks = jnp.cumsum(slot_hits.astype(jnp.int32), axis=0) - 1
    my_rank = jnp.sum(jnp.where(slot_hits, slot_ranks, 0), axis=1)
    sources = my_slot[:, None] * quarters + jnp.arange(quarters, dtype=jnp.int32)[None, :]
    flat_index = jnp.clip(sources * capacity + my_rank[:, None], 0, groups * capacity - 1)
    gathered = jnp.take(
        arrived.reshape(groups * capacity, width), flat_index.reshape(-1), axis=0
    ).reshape(tok_rows, D)
    segment_part = jnp.where(my_in[:, None], gathered.astype(jnp.float32), 0.0)
    slot_place = jnp.where(my_in, my_slot, PACK)
    token_at = (
        jnp.zeros((PACK, capacity), jnp.int32)
        .at[slot_place, my_rank]
        .set(jnp.arange(tok_rows, dtype=jnp.int32), mode="drop")
    )
    valid = jnp.zeros((PACK, capacity), jnp.bool_).at[slot_place, my_rank].set(True, mode="drop")
    grad_pick = jnp.take(whole_grad, token_at.reshape(-1), axis=0).reshape(
        PACK, capacity, quarters, width
    )
    grad_pick = jnp.where(valid[:, :, None, None], grad_pick, jnp.zeros((), jnp.bfloat16))
    grad_send = grad_pick.transpose(0, 2, 1, 3).reshape(groups, capacity, width)
    returned = lax.all_to_all(grad_send, "dp", split_axis=0, concat_axis=0, tiled=True)
    target = jnp.where(filled, row_of, lines)
    accum = (
        jnp.zeros((lines, width), jnp.float32)
        .at[target.reshape(-1)]
        .add(returned.reshape(-1, width).astype(jnp.float32), mode="drop")
    )
    embedded = (
        sum_in_two_steps(segment_part.astype(jnp.bfloat16), "segment")
        .astype(jnp.float32)
        .astype(jnp.bfloat16)
    )
    return (embedded, accum.astype(jnp.bfloat16))


def solution(mesh):
    placed = (P("dp"), P("segment", "dp"), P("dp", "segment"))
    return jax.shard_map(
        body,
        mesh=mesh,
        in_specs=placed,
        out_specs=(P("dp", None), P("segment", "dp")),
        check_vma=False,
    )
```

profile of v0, /device:TPU:1, one launch (start us, length us, event | category | flops | bytes accessed | tf_op | source)
XLA Modules:
  0.0 367.0 jit_solution(8499920811396235449)
XLA Ops:
  7.2 0.0 copy-start
  7.2 1.4 broadcast_in_dim.139
  8.6 15.9 %all-to-all-start = ((s32[32,1,128]{2,1,0:T(1,128)}), s32[32,1,128]{2,1,0:T(1,128)S(1)}, u32[]{:S(2)}, u32[]{:S(2)}) async-start(s32[32,1,128]{2,1,0:T(1,128)} %broadcast_in_dim.139), calls=%async_computation | async-start | bytes 32768 | tf_op jit(solution)/shard_map/all_to_all | solution.py:12
  24.5 11.3 %all-to-all-done = s32[32,1,128]{2,1,0:T(1,128)S(1)} async-done(((s32[32,1,128]{2,1,0:T(1,128)}), s32[32,1,128]{2,1,0:T(1,128)S(1)}, u32[]{:S(2)}, u32[]{:S(2)}) %all-to-all-start) | async-done | bytes 16416 | tf_op jit(solution)/shard_map/all_to_all | solution.py:12
  35.8 2.9 copy.38
  38.7 4.9 %broadcast_compare_fusion = (pred[32,128,1]{2,0,1:T(8,128)(4,1)S(1)}, s32[32,128,1]{2,0,1:T(8,128)S(1)}) fusion(s32[32,128,1]{2,0,1:T(8,128)} %copy.38, s32[]{:T(128)S(6)} %select_n.177), kind=kOutput, calls=%fused_computation.27 | output fusion | flops 667648 | bytes 36868 | tf_op jit(solution)/shard_map/jit(cumsum)/reduce_window_sum | solution.py:59
  43.6 0.0 copy-start.1
  43.6 1.3 copy-done.1
  44.9 1.6 broadcast_add_fusion
  46.5 0.0 copy-start.5
  46.5 2.7 copy.45
  49.2 2.7 copy.44
  51.8 1.5 copy.43
  53.3 0.0 copy-done.5
  53.3 0.1 multiply_reduce_fusion
  53.4 0.0 copy-done.4
  53.4 0.1 and_reduce_fusion
  53.5 15.7 %scatter_custom_fusion.4 = s32[512]{0:T(512)S(1)} fusion(s32[4096]{0:T(1024)S(1)} %get-tuple-element.7, s32[4096]{0:T(1024)S(1)} %get-tuple-element.6, s32[]{:T(128)} %constant.87.clone.1), kind=kCustom, calls=%fused_computation.73 | custom fusion | bytes 2052
  69.2 0.1 reshape.336
  69.3 17.6 %scatter_custom_fusion.3 = pred[512]{0:T(512)(128)(4,1)S(1)} fusion(s32[4096]{0:T(1024)S(1)} %get-tuple-element.7, pred[4096]{0:T(1024)(128)(4,1)S(1)} %broadcast.426, pred[]{:T(512)} %constant.135.clone.1), kind=kCustom, calls=%fused_computation.75 | custom fusion | bytes 513
  86.9 0.1 reshape.332
  87.0 0.1 copy.52
  87.1 0.1 reshape.325
  87.2 0.1 copy.51
  87.3 0.1 copy.50
  87.4 0.0 copy-done
  87.4 2.1 gather_fusion
  89.4 0.0 copy-start.3
  89.4 0.0 copy-start.2
  89.4 1.2 select_select_fusion
  90.6 3.9 %all-to-all-start.1 = ((bf16[32,16,896]{2,1,0:T(8,128)(2,1)}), bf16[32,16,896]{2,1,0:T(8,128)(2,1)S(1)}, u32[]{:S(2)}, u32[]{:S(2)}) async-start(bf16[32,16,896]{2,1,0:T(8,128)(2,1)} %select_select_fusion), calls=%async_computation.1 | async-start | bytes 1835008 | tf_op jit(solution)/shard_map/all_to_all | solution.py:70
  94.5 0.0 copy-done.3
  94.6 0.1 fusion.18
  94.7 0.2 reduce_window_sum.22
  94.9 0.2 select_reduce_fusion
  95.1 6.4 %scatter_fusion.1 = s32[8,16]{1,0:T(8,128)S(1)} fusion(s32[8,16]{1,0:T(8,128)S(1)} %broadcast_in_dim.154, s32[128]{0:T(128)S(1)} %fusion.32, s32[128]{0:T(128)S(1)} %iota.18), kind=kCustom, calls=%fused_computation.4 | custom fusion | bytes 2560 | tf_op jit(solution)/shard_map/scatter | solution.py:87
  101.5 0.1 reshape.328
  101.5 0.0 copy-done.2
  101.6 48.8 %all_gather.7 = bf16[128,3584]{0,1:T(8,128)(2,1)} all-gather(bf16[128,224]{0,1:T(8,128)(2,1)S(1)} %copy-done.2), channel_id=1, replica_groups=mesh['segment'=16,'dp'=32] {'segment'}, dimensions={1}, use_global_device_ids=true | all-gather | bytes 974848 | tf_op jit(solution)/shard_map/all_gather | solution.py:56
  150.4 2.2 copy.54
  152.6 4.3 %gather_fusion.2 = bf16[128,3584]{1,0:T(8,128)(2,1)} fusion(bf16[128,3584]{1,0:T(8,128)(2,1)} %copy.54, s32[1024]{0:T(1024)S(1)} %pad_clamp_fusion), kind=kCustom, calls=%fused_computation.2 | custom fusion | bytes 1835520 | tf_op jit(solution)/shard_map/jit(_take)/gather | solution.py:90
  156.8 2.7 gather.23
  159.5 6.5 %scatter_fusion = pred[8,16]{1,0:T(8,128)(4,1)S(1)} fusion(pred[8,16]{1,0:T(8,128)(4,1)S(1)} %broadcast_in_dim.150, s32[128]{0:T(128)S(1)} %fusion.32, pred[128]{0:T(512)(128)(4,1)S(1)} %broadcast.427), kind=kCustom, calls=%fused_computation.3 | custom fusion | bytes 1408 | tf_op jit(solution)/shard_map/scatter | solution.py:89
  166.0 2.3 fusion.16
  168.4 0.0 all-to-all-done.1
  168.4 37.5 %all-to-all-start.2 = ((bf16[32,16,896]{2,1,0:T(8,128)(2,1)}), bf16[32,16,896]{2,1,0:T(8,128)(2,1)}, u32[]{:S(2)}, u32[]{:S(2)}) async-start(bf16[32,16,896]{2,1,0:T(8,128)(2,1)} %bitcast.56), calls=%async_computation.3 | async-start | bytes 1835008 | tf_op jit(solution)/shard_map/all_to_all | solution.py:95
  205.9 0.3 reduce-scatter.2.cloned.1.call-start
  206.2 0.1 add_clamp_fusion
  206.3 0.1 min.22
  206.4 0.1 compare_and_fusion
  206.5 0.3 broadcast_in_dim.135
  206.8 0.2 copy.58
  207.1 2.7 gather_fusion.1
  209.8 1.7 gather.21
  211.5 1.3 select_convert_fusion
  212.7 0.0 reduce-scatter.2.cloned.1.call-update
  212.8 0.1 copy.53
  212.9 0.1 reshape.327
  212.9 38.2 %all-to-all-done.2 = bf16[32,16,896]{2,1,0:T(8,128)(2,1)} async-done(((bf16[32,16,896]{2,1,0:T(8,128)(2,1)}), bf16[32,16,896]{2,1,0:T(8,128)(2,1)}, u32[]{:S(2)}, u32[]{:S(2)}) %all-to-all-start.2) | async-done | bytes 917536 | tf_op jit(solution)/shard_map/all_to_all | solution.py:95
  251.2 7.6 %scatter_custom_fusion.2 = f32[1188,896]{1,0:T(8,128)} fusion(s32[512]{0:T(512)S(1)} %bitcast.65, f32[]{:T(128)} %constant.145.clone.1, bf16[512,896]{1,0:T(8,128)(2,1)} %bitcast.20), kind=kCustom, calls=%fused_computation.11 | custom fusion | flops 917504 | bytes 5175300 | tf_op jit(solution)/shard_map/scatter-add | solution.py:100
  258.8 3.8 %convert_element_type.34 = bf16[1188,896]{1,0:T(8,128)(2,1)} convert(f32[1188,896]{1,0:T(8,128)} %scatter_custom_fusion.2) | non-fusion elementwise | flops 1064448 | bytes 6386688 | tf_op jit(solution)/shard_map/convert_element_type | solution.py:107
  262.5 52.1 %reduce-scatter.2.cloned.1.call-done = bf16[8,3584]{1,0:T(8,128)(2,1)} async-done(((bf16[128,3584]{1,0:T(8,128)(2,1)}), bf16[8,3584]{1,0:T(8,128)(2,1)}) %reduce-scatter.2.cloned.1.call-update) | async-done | bytes 57360 | tf_op jit(solution)/shard_map/reduce_scatter | solution.py:38
  314.7 44.6 %all_gather.6 = bf16[128,3584]{1,0:T(8,128)(2,1)S(1)} all-gather(bf16[8,3584]{1,0:T(8,128)(2,1)} %reduce-scatter.2.cloned.1.call-done), channel_id=1, replica_groups=mesh['segment'=16,'dp'=32] {'segment'}, dimensions={0}, use_global_device_ids=true | all-gather | bytes 974848 | tf_op jit(solution)/shard_map/all_gather | solution.py:39
  359.3 0.9 copy.65
  (23 shorter events, 0.2 us)
Async XLA Ops:
  7.2 80.2 %copy-start = (bf16[1188,896]{1,0:T(8,128)(2,1)S(1)}, bf16[1188,896]{1,0:T(8,128)(2,1)}, u32[]{:S(2)}) copy-start(bf16[1188,896]{1,0:T(8,128)(2,1)} %param.4) | copy-start | bytes 6386692
  8.6 27.2 %all-to-all-start = ((s32[32,1,128]{2,1,0:T(1,128)}), s32[32,1,128]{2,1,0:T(1,128)S(1)}, u32[]{:S(2)}, u32[]{:S(2)}) async-start(s32[32,1,128]{2,1,0:T(1,128)} %broadcast_in_dim.139), calls=%async_computation | async-start | bytes 32768 | tf_op jit(solution)/shard_map/all_to_all | solution.py:12
  43.6 1.4 copy-start.1
  46.5 6.8 %copy-start.5 = (s32[2]{0:T(128)S(1)}, s32[2]{0:T(128)}, u32[]{:S(2)}) copy-start(s32[2]{0:T(128)} %constant.149) | copy-start | bytes 28
  46.5 6.9 %copy-start.4 = (s32[2]{0:T(128)S(1)}, s32[2]{0:T(128)}, u32[]{:S(2)}) copy-start(s32[2]{0:T(128)} %constant.152) | copy-start | bytes 28
  89.4 5.1 %copy-start.3 = (s32[128]{0:T(128)S(1)}, s32[128]{0:T(128)}, u32[]{:S(2)}) copy-start(s32[128]{0:T(128)} %param.3) | copy-start | bytes 1540
  89.4 12.1 %copy-start.2 = (bf16[128,224]{0,1:T(8,128)(2,1)S(1)}, bf16[128,224]{0,1:T(8,128)(2,1)}, u32[]{:S(2)}) copy-start(bf16[128,224]{0,1:T(8,128)(2,1)} %param.5) | copy-start | bytes 172036
  90.6 77.7 %all-to-all-start.1 = ((bf16[32,16,896]{2,1,0:T(8,128)(2,1)}), bf16[32,16,896]{2,1,0:T(8,128)(2,1)S(1)}, u32[]{:S(2)}, u32[]{:S(2)}) async-start(bf16[32,16,896]{2,1,0:T(8,128)(2,1)} %select_select_fusion), calls=%async_computation.1 | async-start | bytes 1835008 | tf_op jit(solution)/shard_map/all_to_all | solution.py:70
  168.4 82.8 %all-to-all-start.2 = ((bf16[32,16,896]{2,1,0:T(8,128)(2,1)}), bf16[32,16,896]{2,1,0:T(8,128)(2,1)}, u32[]{:S(2)}, u32[]{:S(2)}) async-start(bf16[32,16,896]{2,1,0:T(8,128)(2,1)} %bitcast.56), calls=%async_computation.3 | async-start | bytes 1835008 | tf_op jit(solution)/shard_map/all_to_all | solution.py:95
  205.9 108.8 %reduce-scatter.2.cloned.1.call-start = ((), (), s32[]{:S(2)}) async-start(), calls=%async_computation.4 | async-start | bytes 974848 | tf_op jit(solution)/shard_map/reduce_scatter | solution.py:38
Sparse Core Ops, SparseCore 0:
  212.9 101.7 reduce-scatter.1
where the time goes:
time: 368 us; the launch traced here: 367 us
  waiting for transfers between devices  102 us (28%)
  blocking collectives  93.4 us (25%)
  local copies, waits for them, and re-layouts  76.5 us (21%)
  starting transfers between devices  57.6 us (16%)
  other arithmetic  23.6 us (6%)
  between operations  14.3 us (4%)
    reduce_scatter x1, waiting for transfers between devices, sum_in_two_steps(): own = lax.psum_scatter(padded, axis, scatter_dimension=0, tiled=True)  52.1 us
    all_gather x1, blocking collectives, body(): whole_grad = lax.all_gather(out_grad, 'segment', axis=1, tiled=True)  48.8 us
    all_gather x1, blocking collectives, sum_in_two_steps(): whole = lax.all_gather(own, axis, axis=0, tiled=True)  44.6 us
    all_to_all x1, waiting for transfers between devices, body(): lax.all_to_all(grad_send, 'dp', split_axis=0, concat_axis=0, tiled=True)  38.2 us
    all_to_all x1, starting transfers between devices, body(): lax.all_to_all(grad_send, 'dp', split_axis=0, concat_axis=0, tiled=True)  37.5 us
    unnamed x19, local copies, waits for them, and re-layouts  36 us
    all_to_all x1, starting transfers between devices, copy_for_each(): lax.all_to_all(jnp.broadcast_to(shard[None], (size, *shard.shape)), axis,...  15.9 us
    all_to_all x1, waiting for transfers between devices, copy_for_each(): lax.all_to_all(jnp.broadcast_to(shard[None], (size, *shard.shape)), axis,...  11.3 us
  transfers between devices with their start and end apart: 4, of which 3 were waited for; matrix products, arithmetic and copies ran while one was open for 12% of the time, Pallas kernels for 0%

commit v1 on v0

v1 whole, which is shorter than its diff:
```python
import jax
import jax.numpy as jnp
from jax import lax
from jax.experimental import pallas as pl
from jax.experimental.pallas import tpu as pltpu
from jax.sharding import PartitionSpec as P

MESH = pl.DeviceIdType.MESH
D = 3584
PACK = 8
TOK = 128
GROUPS = 32
X, ZL, ZH, YC = 4, 8, 2, 8
Z = ZH * ZL
LINES = 1188
WIDTH = 896
FEATS = 224
BF = jnp.bfloat16


def coords():
    s = lax.axis_index("segment")
    d = lax.axis_index("dp")
    zh = s // YC
    k = s % YC
    x = d // ZL
    zl = d % ZL
    return zh, k, x, zl


def device(z, k, x):
    return ((z // ZL) * YC + k, x * ZL + z % ZL)


def plane_steps():
    return [(dx, dk) for dx in range(X) for dk in range(YC) if dx or dk]


def first_kernel(ids_ref, piece_ref, all_ref, got_ref, local_sem, id_send, id_recv, ft_send, ft_recv):
    zh, k, x, zl = coords()
    z = zh * ZL + zl
    group = x * ZL + zl
    near = [(dx, dz) for dx in range(X) for dz in range(-3, 5) if dx or dz]

    barrier = pltpu.get_barrier_semaphore()
    for dx, dz in near:
        to = device((z + dz + Z) % Z, k, (x + dx) % X)
        pl.semaphore_signal(barrier, inc=1, device_id=to, device_id_type=MESH)
        if dz == 4:
            back = device((z - dz + Z) % Z, k, (x + dx) % X)
            pl.semaphore_signal(barrier, inc=1, device_id=back, device_id_type=MESH)
    for dk in range(1, YC):
        to = device(z, (k + dk) % YC, x)
        pl.semaphore_signal(barrier, inc=1, device_id=to, device_id_type=MESH)
    own_ids = pltpu.make_async_copy(ids_ref.at[0], all_ref.at[group], local_sem.at[0])
    own_ids.start()
    own_piece = pltpu.make_async_copy(piece_ref.at[k], got_ref.at[k], local_sem.at[1])
    own_piece.start()
    pl.semaphore_wait(barrier, len(near) + X + YC - 1)

    copies = []
    for n, (dx, dz) in enumerate(near):
        copy = pltpu.make_async_remote_copy(
            src_ref=ids_ref.at[0],
            dst_ref=all_ref.at[group],
            send_sem=id_send.at[n],
            recv_sem=id_recv.at[n],
            device_id=device((z + dz + Z) % Z, k, (x + dx) % X),
            device_id_type=MESH,
        )
        copy.start()
        copies.append(copy)
    for dk in range(1, YC):
        other = (k + dk) % YC
        copy = pltpu.make_async_remote_copy(
            src_ref=piece_ref.at[other],
            dst_ref=got_ref.at[k],
            send_sem=ft_send.at[dk],
            recv_sem=ft_recv.at[dk],
            device_id=device(z, other, x),
            device_id_type=MESH,
        )
        copy.start()
        copies.append(copy)
    own_ids.wait()
    own_piece.wait()
    for copy in copies:
        copy.wait()


def vmem(n=1):
    return [pl.BlockSpec(memory_space=pltpu.VMEM)] * n


def first_exchange(ids, piece):
    return pl.pallas_call(
        first_kernel,
        out_shape=(
            jax.ShapeDtypeStruct((GROUPS, 1, TOK), jnp.int32),
            jax.ShapeDtypeStruct((YC, 16, FEATS), BF),
        ),
        in_specs=vmem(2),
        out_specs=tuple(vmem(2)),
        scratch_shapes=[
            pltpu.SemaphoreType.DMA((2,)),
            pltpu.SemaphoreType.DMA((GROUPS - 1,)),
            pltpu.SemaphoreType.DMA((GROUPS - 1,)),
            pltpu.SemaphoreType.DMA((YC,)),
            pltpu.SemaphoreType.DMA((YC,)),
        ],
        compiler_params=pltpu.CompilerParams(collective_id=0, has_side_effects=True),
        name="first",
    )(ids, piece)


def onehot(condition):
    return jnp.where(condition, jnp.float32(1), jnp.float32(0)).astype(BF)


def dot(a, b):
    return jnp.dot(a, b, preferred_element_type=jnp.float32).astype(BF)


def main_kernel(
    lcol_ref, lrow_ref, mcol_ref, mrow_ref, pos_ref, table_ref, grad_ref,
    emb_ref, tg_ref,
    es, er, dr, gs, gr, de, zr, fr, fs,
    local_sem, ab_send, ab_recv, zt_send, zt_recv, bt_send, bt_recv, z_send, z_recv, f_send, f_recv,
):
    zh, k, x, zl = coords()
    z = zh * ZL + zl
    me = x * YC + k
    plane = plane_steps()

    barrier = pltpu.get_barrier_semaphore()
    for dx, dk in plane:
        to = device(z, (k + dk) % YC, (x + dx) % X)
        pl.semaphore_signal(barrier, inc=1, device_id=to, device_id_type=MESH)
    for dz in range(1, Z):
        to = device((z + dz) % Z, k, x)
        pl.semaphore_signal(barrier, inc=1, device_id=to, device_id_type=MESH)

    def pick_rows(i, carry):
        rows = pl.ds(pl.multiple_of(i * TOK, TOK), TOK)
        pick = onehot(lcol_ref[rows, :] == lax.broadcasted_iota(jnp.int32, (TOK, LINES), 1))
        es[pl.ds(i * 8, 8)] = dot(pick, table_ref[...]).reshape(8, 16, WIDTH)
        return carry

    lax.fori_loop(0, 4, pick_rows, 0)

    pl.semaphore_wait(barrier, len(plane) + Z - 1)

    def plane_copies(src, dst, send, recv):
        out = []
        for n, (dx, dk) in enumerate(plane):
            ox, ok = (x + dx) % X, (k + dk) % YC
            copy = pltpu.make_async_remote_copy(
                src_ref=src.at[ox * YC + ok],
                dst_ref=dst.at[me],
                send_sem=send.at[n],
                recv_sem=recv.at[n],
                device_id=device(z, ok, ox),
                device_id_type=MESH,
            )
            copy.start()
            out.append(copy)
        return out

    ab = plane_copies(es, er, ab_send, ab_recv)
    own_ab = pltpu.make_async_copy(es.at[me], er.at[me], local_sem.at[0])
    own_ab.start()

    zt = []
    for h in range(2):
        for m in range(4):
            there = 2 * zh + h + 4 * m
            copy = pltpu.make_async_remote_copy(
                src_ref=grad_ref.at[h],
                dst_ref=dr.at[zl],
                send_sem=zt_send.at[h * 4 + m],
                recv_sem=zt_recv.at[zl],
                device_id=device(there, k, x),
                device_id_type=MESH,
            )
            zt.append((there, copy))
            own = pltpu.make_async_copy(grad_ref.at[h], dr.at[zl], local_sem.at[1])

            @pl.when(there != z)
            def _():
                copy.start()

            @pl.when(there == z)
            def _():
                own.start()
                own.wait()

    q = zl % 4
    from_z = (q // 2) * ZL
    for zg in range(ZL):
        @pl.when(from_z + zg != z)
        def _():
            pltpu.make_async_remote_copy(
                src_ref=grad_ref.at[0],
                dst_ref=dr.at[zg],
                send_sem=zt_send.at[0],
                recv_sem=zt_recv.at[zg],
                device_id=device(z, k, x),
                device_id_type=MESH,
            ).wait_recv()

    spread = onehot(
        lax.broadcasted_iota(jnp.int32, (512, TOK), 0) == mrow_ref[...]
    )
    gs[...] = dot(spread, dr[...].reshape(TOK, WIDTH)).reshape(GROUPS, 16, WIDTH)
    bt = plane_copies(gs, gr, bt_send, bt_recv)
    own_bt = pltpu.make_async_copy(gs.at[me], gr.at[me], local_sem.at[2])
    own_bt.start()

    own_ab.wait()
    for copy in ab:
        copy.wait_recv()
    merge = onehot(mcol_ref[...] == lax.broadcasted_iota(jnp.int32, (TOK, 512), 1))
    de[...] = dot(merge, er[...].reshape(512, WIDTH)).reshape(ZL, 16, WIDTH)

    own_z = pltpu.make_async_copy(de.at[zl], zr.at[z], local_sem.at[3])
    own_z.start()
    zc = []
    for dz in range(1, Z):
        there = (z + dz) % Z
        copy = pltpu.make_async_remote_copy(
            src_ref=de.at[there % ZL],
            dst_ref=zr.at[z],
            send_sem=z_send.at[dz],
            recv_sem=z_recv.at[dz],
            device_id=device(there, k, x),
            device_id_type=MESH,
        )
        copy.start()
        zc.append(copy)

    own_bt.wait()
    for copy in bt:
        copy.wait_recv()

    def scatter(start, rows):
        line = start + lax.broadcasted_iota(jnp.int32, (rows, 512), 0)
        place = onehot(line == lrow_ref[...])
        tg_ref[pl.ds(start, rows), :] = dot(place, gr[...].reshape(512, WIDTH))

    def scatter_step(i, carry):
        scatter(pl.multiple_of(i * TOK, TOK), TOK)
        return carry

    lax.fori_loop(0, LINES // TOK, scatter_step, 0)
    scatter(LINES // TOK * TOK, LINES % TOK)

    own_z.wait()
    for copy in zc:
        copy.wait_recv()
    for quarter in range(4):
        total = (
            zr[quarter].astype(jnp.float32)
            + zr[quarter + 4].astype(jnp.float32)
            + zr[quarter + 8].astype(jnp.float32)
            + zr[quarter + 12].astype(jnp.float32)
        )
        fs[:, quarter * WIDTH : (quarter + 1) * WIDTH] = total.astype(BF)

    own_f = pltpu.make_async_copy(fs, fr.at[k], local_sem.at[4])
    own_f.start()
    fc = []
    for dk in range(1, YC):
        copy = pltpu.make_async_remote_copy(
            src_ref=fs,
            dst_ref=fr.at[k],
            send_sem=f_send.at[dk],
            recv_sem=f_recv.at[dk],
            device_id=device(z, (k + dk) % YC, x),
            device_id_type=MESH,
        )
        copy.start()
        fc.append(copy)
    own_f.wait()
    for copy in fc:
        copy.wait_recv()
    back = onehot(pos_ref[...] == lax.broadcasted_iota(jnp.int32, (TOK, TOK), 1))
    emb_ref[...] = dot(back, fr[...].reshape(TOK, D))

    for copy in ab + bt + zc + fc:
        copy.wait_send()
    for there, copy in zt:
        @pl.when(there != z)
        def _():
            copy.wait_send()


def main_exchange(lcol, lrow, mcol, mrow, pos, table, grad):
    dma = pltpu.SemaphoreType.DMA
    return pl.pallas_call(
        main_kernel,
        out_shape=(
            jax.ShapeDtypeStruct((TOK, D), BF),
            jax.ShapeDtypeStruct((LINES, WIDTH), BF),
        ),
        in_specs=vmem(7),
        out_specs=tuple(vmem(2)),
        scratch_shapes=[
            pltpu.VMEM((GROUPS, 16, WIDTH), BF),
            pltpu.VMEM((GROUPS, 16, WIDTH), BF),
            pltpu.VMEM((ZL, 16, WIDTH), BF),
            pltpu.VMEM((GROUPS, 16, WIDTH), BF),
            pltpu.VMEM((GROUPS, 16, WIDTH), BF),
            pltpu.VMEM((ZL, 16, WIDTH), BF),
            pltpu.VMEM((Z, 16, WIDTH), BF),
            pltpu.VMEM((YC, 16, D), BF),
            pltpu.VMEM((16, D), BF),
            dma((5,)),
            dma((31,)), dma((31,)),
            dma((8,)), dma((8,)),
            dma((31,)), dma((31,)),
            dma((16,)), dma((16,)),
            dma((8,)), dma((8,)),
        ],
        compiler_params=pltpu.CompilerParams(
            collective_id=1, has_side_effects=True, vmem_limit_bytes=48 * 1024 * 1024
        ),
        name="main",
    )(lcol, lrow, mcol, mrow, pos, table, grad)


def sorted_places(ids):
    bucket = ids // (LINES * PACK) * PACK + ids % PACK
    at = jnp.arange(TOK, dtype=jnp.int32)
    key = bucket * TOK + at
    less = key[:, None, :] < key[:, :, None]
    same = bucket[:, None, :] == bucket[:, :, None]
    place = jnp.sum(less.astype(jnp.int32), axis=2)
    rank = jnp.sum((less & same).astype(jnp.int32), axis=2)
    return bucket, place, rank


def body(token_ids, table, out_grad):
    zh, k, x, zl = coords()
    parity = zl // 4
    steps16 = jnp.arange(16, dtype=jnp.int32)

    _, own_place, _ = sorted_places(token_ids[None])
    own_place = own_place[0]
    pos = own_place % 8 * 16 + own_place // 8
    order = onehot(jnp.arange(TOK, dtype=jnp.int32)[:, None] == pos[None, :])
    piece = dot(order, out_grad).reshape(YC, 16, FEATS)

    all_ids, got = first_exchange(token_ids.reshape(1, 1, TOK), piece)
    grad = got.reshape(2, 4, 16, FEATS).transpose(0, 2, 1, 3).reshape(2, 16, WIDTH)

    ids = all_ids.reshape(GROUPS, TOK)
    bucket, place, rank = sorted_places(ids)
    line = ids % (LINES * PACK) // PACK
    slot = 2 * x + parity
    mine = bucket == (zh * YC + k) * PACK + slot
    code = jnp.where(mine, place % 8 * 2 + rank // 8, -1)
    found = jnp.sum(
        jnp.where(code[:, None, :] == steps16[None, :, None], line[:, None, :] + 1, 0), axis=2
    ) - 1
    wanted = found.reshape(X, ZL, YC, 2).transpose(0, 2, 1, 3).reshape(512)

    def of_mine(a):
        return lax.dynamic_slice_in_dim(a, x * ZL, ZL, 0)

    near_bucket, near_place, near_rank = of_mine(bucket), of_mine(place), of_mine(rank)
    segment, owner_slot = near_bucket // PACK, near_bucket % PACK
    here = (segment // YC == zh) & (owner_slot % 2 == parity)
    source = (owner_slot // 2 * YC + segment % YC) * 16 + near_rank // 8
    source = source + 2 * jnp.arange(ZL, dtype=jnp.int32)[:, None]
    value = jnp.where(here, source + 1, 0)
    at = near_place[:, None, :] == (steps16 * 8 + k)[None, :, None]
    merged = (jnp.sum(jnp.where(at, value[:, None, :], 0), axis=2) - 1).reshape(TOK)

    return main_exchange(
        wanted[:, None], wanted[None, :], merged[:, None], merged[None, :], pos[:, None], table, grad
    )


def solution(mesh):
    return jax.shard_map(
        body,
        mesh=mesh,
        in_specs=(P("dp"), P("segment", "dp"), P("dp", "segment")),
        out_specs=(P("dp", None), P("segment", "dp")),
        check_vma=False,
    )
```

time: 368 us -> 95.7 us (0.26)
  waiting for transfers between devices: 102 us -> 0 us
  blocking collectives: 93.4 us -> 0 us
  Pallas kernels: 0 us -> 82.9 us
  local copies, waits for them, and re-layouts: 76.5 us -> 4.94 us
  starting transfers between devices: 57.6 us -> 0 us
  other arithmetic: 23.6 us -> 6.49 us
  between operations: 14.3 us -> 0.85 us
    all_gather x2 -> x0, blocking collectives: 93.4 us -> none  [the longest x1 48.8 us: body(): whole_grad = lax.all_gather(out_grad, 'segment', axis=1, tiled=True)]
    pallas_call x0 -> x2, Pallas kernels: none -> 82.9 us  [the longest x1 60.3 us: main_exchange(): pl.pallas_call(main_kernel, out_shape=(jax.ShapeDtypeStruct((TOK, D), BF)...]
    all_to_all x3 -> x0, starting transfers between devices: 57.4 us -> none  [the longest x1 37.5 us: body(): lax.all_to_all(grad_send, 'dp', split_axis=0, concat_axis=0, tiled=True)]
    reduce_scatter x1 -> x0, waiting for transfers between devices: 52.1 us -> none  [sum_in_two_steps(): own = lax.psum_scatter(padded, axis, scatter_dimension=0, tiled=True)]
    all_to_all x3 -> x0, waiting for transfers between devices: 49.5 us -> none  [the longest x1 38.2 us: body(): lax.all_to_all(grad_send, 'dp', split_axis=0, concat_axis=0, tiled=True)]
    unnamed x19 -> x6, local copies, waits for them, and re-layouts: 36 us -> 2.27 us
    gather x5 -> x0, local copies, waits for them, and re-layouts: 13.4 us -> none  [the longest x2 6.91 us: body(): jnp.take(whole_grad, token_at.reshape(-1), axis=0)]
    scatter x4 -> x0, local copies, waits for them, and re-layouts: 13 us -> none  [the longest x1 6.48 us: body(): jnp.zeros((PACK, capacity), jnp.bool_).at[slot_place, my_rank]]
  transfers between devices with their start and end apart: 4 -> 0, of which waited for: 3 -> 0; matrix products, arithmetic and copies ran while one was open for 12% -> 0% of each run, Pallas kernels for 0% -> 0%
where the time goes in v1:
time: 95.7 us; the launch traced here: 95.3 us
  Pallas kernels  82.9 us (87%)
  other arithmetic  6.49 us (7%)
  local copies, waits for them, and re-layouts  4.94 us (5%)
    pallas_call x1, Pallas kernels, main_exchange(): pl.pallas_call(main_kernel, out_shape=(jax.ShapeDtypeStruct((TOK, D), BF)...  60.3 us
    pallas_call x1, Pallas kernels, first_exchange(): pl.pallas_call(first_kernel, out_shape=(jax.ShapeDtypeStruct((GROUPS, 1,...  22.5 us
    reduce_sum x1, other arithmetic, sorted_places(): rank = jnp.sum((less & same).astype(jnp.int32), axis=2)  2.59 us
    add x3, other arithmetic, sorted_places(): key = bucket * TOK + at  2.53 us
    unnamed x6, local copies, waits for them, and re-layouts  2.27 us

profile of v1, /device:TPU:1, one launch (start us, length us, event | category | flops | bytes accessed | tf_op | source)
XLA Modules:
  0.0 95.3 jit_solution(16032132807673490849)
XLA Ops:
  0.6 0.0 copy-start
  0.6 0.0 copy-start.1
  0.7 0.8 iota_add_fusion.2
  1.5 0.2 convert_reduce_fusion.1
  1.8 0.0 copy-done
  1.8 0.2 convolution_convert_fusion
  1.9 0.7 copy.45
  2.7 22.5 %first.1 = (s32[32,1,128]{2,1,0:T(1,128)}, bf16[8,16,224]{2,1,0:T(8,128)(2,1)}) custom-call(s32[1,1,128]{2,1,0:T(1,128)} %bitcast.33, bf16[8,16,224]{2,1,0:T(8,128)(2,1)} %bitcast.22), custom_call_target="tpu_custom_call" | custom-call | tf_op jit(solution)/shard_map/first/pallas_call | solution.py:96
  25.2 0.9 copy.57
  26.1 0.1 reshape.397.grad_ref
  26.2 0.7 iota_add_fusion
  27.0 1.0 %iota_add_fusion.1 = (s32[32,1,128]{2,1,0:T(1,128)S(1)}, s32[32,1,128]{2,1,0:T(1,128)S(1)}, s32[32,1,128]{2,1,0:T(1,128)S(1)}) fusion(s32[32,1,128]{2,1,0:T(1,128)} %get-tuple-element.4), kind=kLoop, calls=%fused_computation.60 | loop fusion | flops 176128 | bytes 65536 | tf_op jit(solution)/shard_map/add | solution.py:334
  27.9 2.6 %convert_reduce_fusion = (s32[32,128]{1,0:T(8,128)S(1)}, s32[32,128]{1,0:T(8,128)S(1)}) fusion(s32[32,128]{1,0:T(8,128)S(1)} %get-tuple-element.11, s32[32,128]{1,0:T(8,128)S(1)} %bitcast.24, s32[32,128]{1,0:T(8,128)S(1)} %get-tuple-element.10, s32[32,128]{1,0:T(8,128)S(1)} %bitcast.32), kind=kLoop, calls=%fused_computation.3 | loop fusion | flops 3661824 | bytes 98304 | tf_op jit(solution)/shard_map/reduce_sum | solution.py:338
  30.5 0.1 fusion.29
  30.6 0.3 select_reduce_fusion.1
  30.9 0.1 compare_select_fusion.4
  31.0 0.6 select_reduce_fusion
  31.7 0.1 copy.46
  31.7 0.1 sub.89.mrow_ref
  31.8 0.1 sub.82
  31.9 0.1 sub.91.mcol_ref
  32.0 0.1 copy.49
  32.1 0.1 fusion.2.pos_ref
  32.2 0.3 copy.47
  32.4 0.1 broadcast_in_dim_reshape.9.lrow_ref
  32.6 0.1 broadcast_in_dim_reshape.10.lcol_ref
  32.7 0.0 copy-done.1
  32.7 60.3 %main.1 = (bf16[128,3584]{1,0:T(8,128)(2,1)S(1)}, bf16[1188,896]{1,0:T(8,128)(2,1)S(1)}) custom-call(s32[512,1]{1,0:T(8,128)S(1)} %broadcast_in_dim_reshape.10.lcol_ref, s32[1,512]{1,0:T(1,128)S(1)} %broadcast_in_dim_reshape.9.lrow_ref, s32[128,1]{1,0:T(8,128)S(1)} %sub.91.mcol_ref, s32[1,128]{1,0:T(1,128)S(1)} %sub.89.mrow_ref, ...), custom_call_target="tpu_custom_call" | custom-call | tf_op jit(solution)/shard_map/main/pallas_call | solution.py:299
  93.1 0.9 copy.60
  94.0 1.3 %copy.61 = bf16[1188,896]{1,0:T(8,128)(2,1)} copy(bf16[1188,896]{1,0:T(8,128)(2,1)S(1)} %get-tuple-element.18) | data formatting | bytes 4257792
  (5 shorter events, 0.0 us)
Async XLA Ops:
  0.6 1.1 %copy-start = (bf16[128,224]{0,1:T(8,128)(2,1)S(1)}, bf16[128,224]{0,1:T(8,128)(2,1)}, u32[]{:S(2)}) copy-start(bf16[128,224]{0,1:T(8,128)(2,1)} %param.5) | copy-start | bytes 172036
  0.6 32.1 %copy-start.1 = (bf16[1188,896]{1,0:T(8,128)(2,1)S(1)}, bf16[1188,896]{1,0:T(8,128)(2,1)}, u32[]{:S(2)}) copy-start(bf16[1188,896]{1,0:T(8,128)(2,1)} %table_ref.1) | copy-start | bytes 6386692

commit v2 on v0

v2 whole, which is shorter than its diff:
```python
import jax
import jax.numpy as jnp
from jax import lax
from jax.experimental import pallas as pl
from jax.experimental.pallas import tpu as pltpu
from jax.sharding import PartitionSpec as P

MESH = pl.DeviceIdType.MESH
D = 3584
PACK = 8
TOK = 128
GROUPS = 32
X, ZL, ZH, YC = 4, 8, 2, 8
Z = ZH * ZL
LINES = 1188
WIDTH = 896
FEATS = 224
BF = jnp.bfloat16
F32 = jnp.float32
CUTS = (256, 384, 256)
STARTS = (0, 256, 640)


def coords():
    s = lax.axis_index("segment")
    d = lax.axis_index("dp")
    zh = s // YC
    k = s % YC
    x = d // ZL
    zl = d % ZL
    return zh, k, x, zl


def device(z, k, x):
    return ((z // ZL) * YC + k, x * ZL + z % ZL)


def plane_steps():
    return [(dx, dk) for dx in range(X) for dk in range(YC) if dx or dk]


def vmem(n=1):
    return [pl.BlockSpec(memory_space=pltpu.VMEM)] * n


def onehot(condition):
    return jnp.where(condition, F32(1), F32(0)).astype(BF)


def dot(a, b):
    return jnp.dot(a, b, preferred_element_type=F32).astype(BF)


def iota(shape, dim):
    return lax.broadcasted_iota(jnp.int32, shape, dim).astype(F32)


def remote(src, dst, send, recv, to):
    copy = pltpu.make_async_remote_copy(
        src_ref=src, dst_ref=dst, send_sem=send, recv_sem=recv, device_id=to, device_id_type=MESH
    )
    copy.start()
    return copy


def local(src, dst, sem):
    copy = pltpu.make_async_copy(src, dst, sem)
    copy.start()
    return copy


def settle(ref, sem):
    pltpu.make_async_copy(ref, ref, sem).wait()


def whole_kernel(
    ids_ref, table_hbm, gradt_ref, emb_ref, tg_ref,
    table, info, mine, piece, got, place_at, gq, order_ref, s_ref, lrow_ref,
    es0, es1, es2, er0, er1, er2, dr, gs, gr, de0, de1, de2, zr0, zr1, zr2,
    fs0, fs1, fs2, fr0, fr1, fr2,
    table_sem, id_send, id_recv, ft_send, ft_recv, zt_send, zt_recv,
    ab_send, ab_recv, bt_send, bt_recv, z_send, z_recv, f_send, f_recv,
):
    es, er, de, zr = (es0, es1, es2), (er0, er1, er2), (de0, de1, de2), (zr0, zr1, zr2)
    fs, fr = (fs0, fs1, fs2), (fr0, fr1, fr2)
    zh, k, x, zl = coords()
    z = zh * ZL + zl
    me = x * YC + k
    group = x * ZL + zl
    parity = zl // 4
    plane = plane_steps()
    near = [(dx, dz) for dx in range(X) for dz in range(-4, 5) if dz]

    barrier = pltpu.get_barrier_semaphore()
    for dx, dz in near:
        to = device((z + dz + Z) % Z, k, (x + dx) % X)
        pl.semaphore_signal(barrier, inc=1, device_id=to, device_id_type=MESH)
    for dx, dk in plane:
        to = device(z, (k + dk) % YC, (x + dx) % X)
        pl.semaphore_signal(barrier, inc=1, device_id=to, device_id_type=MESH)
    table_copy = local(table_hbm, table, table_sem)

    ids = ids_ref[...]
    segment = ((ids.astype(F32) + 0.5) * F32(1.0 / (LINES * PACK))).astype(jnp.int32)
    slot = ids & 7
    line = (ids - segment * (LINES * PACK)) >> 3
    bucket = segment * PACK + slot
    key = (bucket * TOK + lax.broadcasted_iota(jnp.int32, (1, TOK), 1)).astype(F32)
    keys = jnp.broadcast_to(key, (TOK, TOK))
    turned = keys.T
    first = (bucket * TOK).astype(F32)
    at = jnp.sum(jnp.where(turned < keys, F32(1), F32(0)), axis=0, keepdims=True)
    begin = jnp.sum(jnp.where(turned < first, F32(1), F32(0)), axis=0, keepdims=True)
    at = at.astype(jnp.int32)
    second = (at - begin.astype(jnp.int32)) >> 3
    klass, inside = at & 7, at >> 3
    rows = (
        line + 1,
        bucket,
        klass * 16 + second,
        klass,
        inside,
        ((slot >> 1) * YC + (segment & 7)) * 16 + second,
        (segment >> 3) * 2 + (slot & 1),
        slot,
    )
    for n, row in enumerate(rows):
        mine[n : n + 1, :] = row.astype(F32)
    order = jnp.where(
        iota((TOK, TOK), 0) == (klass * 16 + inside).astype(F32), F32(1), F32(0)
    )
    order_ref[...] = order.T.astype(BF)
    sorted_grad = lax.dot_general(
        order.astype(BF), gradt_ref[...], (((1,), (1,)), ((), ())), preferred_element_type=F32
    ).astype(BF)
    piece[...] = sorted_grad.reshape(YC, 16, FEATS)
    for j in range(4):
        place_at[j] = onehot(iota((FEATS, WIDTH), 0) + F32(FEATS * j) == iota((FEATS, WIDTH), 1))

    pl.semaphore_wait(barrier, len(near) + len(plane))

    for dx, dz in [(dx, dz) for dx in range(X) for dz in range(-3, 5) if dx or dz]:
        remote(mine, info.at[group], id_send, id_recv, device((z + dz + Z) % Z, k, (x + dx) % X))
    local(mine, info.at[group], id_recv)
    for dk in range(1, YC):
        other = (k + dk) % YC
        remote(piece.at[other], got.at[k], ft_send, ft_recv, device(z, other, x))
    local(piece.at[k], got.at[k], ft_recv)

    settle(got, ft_recv)
    for h in range(2):
        total = jnp.zeros((16, WIDTH), F32)
        for j in range(4):
            total = total + jnp.dot(got[4 * h + j], place_at[j], preferred_element_type=F32)
        gq[h] = total.astype(BF)
    settle(info, id_recv)

    zt = []
    for h in range(2):
        for m in range(4):
            there = 2 * zh + h + 4 * m
            copy = pltpu.make_async_remote_copy(
                src_ref=gq.at[h],
                dst_ref=dr.at[zl],
                send_sem=zt_send.at[h * 4 + m],
                recv_sem=zt_recv,
                device_id=device(there, k, x),
                device_id_type=MESH,
            )
            zt.append((there, copy))

            @pl.when(there != z)
            def _():
                copy.start()

            @pl.when(there == z)
            def _():
                local(gq.at[h], dr.at[zl], zt_recv)

    sub = iota((TOK, TOK), 0)
    my_bucket = ((zh * YC + k) * PACK + 2 * x + parity).astype(F32)
    for ox in range(X):
        acc = jnp.zeros((TOK, TOK), F32)
        for zg in range(ZL):
            rows = info[ox * ZL + zg]
            code = jnp.where(rows[1:2] == my_bucket, rows[2:3] + F32(2 * zg), F32(-1))
            acc = acc + jnp.where(sub == code, rows[0:1], F32(0))
        lcol = jnp.sum(acc, axis=1, keepdims=True) - 1
        lrow_ref[:, ox * TOK : (ox + 1) * TOK] = jnp.sum(acc.T, axis=0, keepdims=True) - 1
        s_ref[ox * TOK : (ox + 1) * TOK, :] = onehot(lcol == iota((TOK, LINES), 1))
    table_copy.wait()

    def plane_copies(src, dst, send, recv):
        for dx, dk in plane:
            ox, ok = (x + dx) % X, (k + dk) % YC
            remote(src.at[ox * YC + ok], dst.at[me], send, recv, device(z, ok, ox))
        local(src.at[me], dst.at[me], recv)

    for c, (start, width) in enumerate(zip(STARTS, CUTS)):
        def pick_rows(i, carry):
            rows = pl.ds(pl.multiple_of(i * TOK, TOK), TOK)
            picked = dot(s_ref[rows, :], table[:, start : start + width])
            es[c][pl.ds(i * 8, 8)] = picked.reshape(8, 16, width)
            return carry

        lax.fori_loop(0, 4, pick_rows, 0)
        plane_copies(es[c], er[c], ab_send.at[c], ab_recv.at[c])

    acc = jnp.zeros((TOK, TOK), F32)
    my_half = (zh * 2 + parity).astype(F32)
    my_class = k.astype(F32)
    for zg in range(ZL):
        rows = info[x * ZL + zg]
        here = (rows[3:4] == my_class) & (rows[6:7] == my_half)
        code = jnp.where(here, rows[4:5] + F32(16 * zg), F32(-1))
        acc = acc + jnp.where(sub == code, rows[5:6] + F32(2 * zg + 1), F32(0))
    mcol = jnp.sum(acc, axis=1, keepdims=True) - 1
    mrow = jnp.sum(acc.T, axis=0, keepdims=True) - 1
    merge = onehot(mcol == iota((TOK, 512), 1))
    spread = onehot(iota((512, TOK), 0) == mrow)

    def merge_and_send(c):
        settle(er[c], ab_recv.at[c])
        de[c][...] = dot(merge, er[c][...].reshape(512, CUTS[c])).reshape(ZL, 16, CUTS[c])
        for dz in range(1, Z):
            there = (z + dz) % Z
            remote(de[c].at[there % ZL], zr[c].at[z], z_send.at[c], z_recv.at[c], device(there, k, x))
        local(de[c].at[zl], zr[c].at[z], z_recv.at[c])

    merge_and_send(0)
    settle(dr, zt_recv)
    gs[...] = dot(spread, dr[...].reshape(TOK, WIDTH)).reshape(GROUPS, 16, WIDTH)
    merge_and_send(1)
    plane_copies(gs, gr, bt_send, bt_recv)
    merge_and_send(2)

    def sum_and_send(c):
        settle(zr[c], z_recv.at[c])
        for quarter in range(4):
            total = zr[c][quarter].astype(F32)
            for m in range(1, 4):
                total = total + zr[c][quarter + 4 * m].astype(F32)
            fs[c][quarter] = total.astype(BF)
        for dk in range(1, YC):
            remote(fs[c], fr[c].at[k], f_send.at[c], f_recv.at[c], device(z, (k + dk) % YC, x))
        local(fs[c], fr[c].at[k], f_recv.at[c])

    def finish(c):
        settle(fr[c], f_recv.at[c])
        for quarter in range(4):
            start = quarter * WIDTH + STARTS[c]
            rows = fr[c][:, quarter].reshape(TOK, CUTS[c])
            emb_ref[:, start : start + CUTS[c]] = dot(order_ref[...], rows)

    sum_and_send(0)
    sum_and_send(1)
    settle(gr, bt_recv)

    def scatter(start, rows):
        line = (start + lax.broadcasted_iota(jnp.int32, (rows, 512), 0)).astype(F32)
        place = onehot(line == lrow_ref[...])
        tg_ref[pl.ds(start, rows), :] = dot(place, gr[...].reshape(512, WIDTH))

    def scatter_step(i, carry):
        scatter(pl.multiple_of(i * TOK, TOK), TOK)
        return carry

    lax.fori_loop(0, LINES // TOK, scatter_step, 0)
    scatter(LINES // TOK * TOK, LINES % TOK)
    finish(0)
    sum_and_send(2)
    finish(1)
    finish(2)

    settle(info.at[pl.ds(0, GROUPS - 1)], id_send)
    settle(got.at[pl.ds(0, YC - 1)], ft_send)
    settle(gr.at[pl.ds(0, GROUPS - 1)], bt_send)
    for c in range(3):
        settle(er[c].at[pl.ds(0, GROUPS - 1)], ab_send.at[c])
        settle(zr[c].at[pl.ds(0, Z - 1)], z_send.at[c])
        settle(fr[c].at[pl.ds(0, YC - 1)], f_send.at[c])
    for there, copy in zt:
        @pl.when(there != z)
        def _():
            copy.wait_send()


def body(token_ids, table, out_grad):
    dma = pltpu.SemaphoreType.DMA

    def each(*lead):
        return [pltpu.VMEM((*lead, width), BF) for width in CUTS]

    return pl.pallas_call(
        whole_kernel,
        out_shape=(
            jax.ShapeDtypeStruct((TOK, D), BF),
            jax.ShapeDtypeStruct((LINES, WIDTH), BF),
        ),
        in_specs=[vmem()[0], pl.BlockSpec(memory_space=pl.ANY), vmem()[0]],
        out_specs=tuple(vmem(2)),
        scratch_shapes=[
            pltpu.VMEM((LINES, WIDTH), BF),
            pltpu.VMEM((GROUPS, 8, TOK), F32),
            pltpu.VMEM((8, TOK), F32),
            pltpu.VMEM((YC, 16, FEATS), BF),
            pltpu.VMEM((YC, 16, FEATS), BF),
            pltpu.VMEM((4, FEATS, WIDTH), BF),
            pltpu.VMEM((2, 16, WIDTH), BF),
            pltpu.VMEM((TOK, TOK), BF),
            pltpu.VMEM((512, LINES), BF),
            pltpu.VMEM((1, 512), F32),
            *each(GROUPS, 16),
            *each(GROUPS, 16),
            pltpu.VMEM((ZL, 16, WIDTH), BF),
            pltpu.VMEM((GROUPS, 16, WIDTH), BF),
            pltpu.VMEM((GROUPS, 16, WIDTH), BF),
            *each(ZL, 16),
            *each(Z, 16),
            *each(4, 16),
            *each(YC, 4, 16),
            dma, dma, dma, dma, dma, dma((8,)), dma,
            dma((3,)), dma((3,)), dma, dma, dma((3,)), dma((3,)), dma((3,)), dma((3,)),
        ],
        compiler_params=pltpu.CompilerParams(
            collective_id=0, has_side_effects=True, vmem_limit_bytes=48 * 1024 * 1024
        ),
        name="whole",
    )(token_ids.reshape(1, TOK), table, out_grad.T)


def solution(mesh):
    return jax.shard_map(
        body,
        mesh=mesh,
        in_specs=(P("dp"), P("segment", "dp"), P("dp", "segment")),
        out_specs=(P("dp", None), P("segment", "dp")),
        check_vma=False,
    )
```

time: 368 us -> 70.1 us (0.19)
  waiting for transfers between devices: 102 us -> 0 us
  blocking collectives: 93.4 us -> 0 us
  local copies, waits for them, and re-layouts: 76.5 us -> 5.33 us
  Pallas kernels: 0 us -> 64 us
  starting transfers between devices: 57.6 us -> 0 us
  other arithmetic: 23.6 us -> 0 us
  between operations: 14.3 us -> 0.65 us
    all_gather x2 -> x0, blocking collectives: 93.4 us -> none  [the longest x1 48.8 us: body(): whole_grad = lax.all_gather(out_grad, 'segment', axis=1, tiled=True)]
    pallas_call x0 -> x1, Pallas kernels: none -> 64 us  [body(): pl.pallas_call(whole_kernel, out_shape=(jax.ShapeDtypeStruct((TOK, D), BF...]
    all_to_all x3 -> x0, starting transfers between devices: 57.4 us -> none  [the longest x1 37.5 us: body(): lax.all_to_all(grad_send, 'dp', split_axis=0, concat_axis=0, tiled=True)]
    reduce_scatter x1 -> x0, waiting for transfers between devices: 52.1 us -> none  [sum_in_two_steps(): own = lax.psum_scatter(padded, axis, scatter_dimension=0, tiled=True)]
    all_to_all x3 -> x0, waiting for transfers between devices: 49.5 us -> none  [the longest x1 38.2 us: body(): lax.all_to_all(grad_send, 'dp', split_axis=0, concat_axis=0, tiled=True)]
    unnamed x19 -> x8, local copies, waits for them, and re-layouts: 36 us -> 5.33 us
    gather x5 -> x0, local copies, waits for them, and re-layouts: 13.4 us -> none  [the longest x2 6.91 us: body(): jnp.take(whole_grad, token_at.reshape(-1), axis=0)]
    scatter x4 -> x0, local copies, waits for them, and re-layouts: 13 us -> none  [the longest x1 6.48 us: body(): jnp.zeros((PACK, capacity), jnp.bool_).at[slot_place, my_rank]]
  transfers between devices with their start and end apart: 4 -> 0, of which waited for: 3 -> 0; matrix products, arithmetic and copies ran while one was open for 12% -> 0% of each run, Pallas kernels for 0% -> 0%
where the time goes in v2:
time: 70.1 us; the launch traced here: 69.9 us
  Pallas kernels  64 us (91%)
  local copies, waits for them, and re-layouts  5.33 us (8%)
    pallas_call x1, Pallas kernels, body(): pl.pallas_call(whole_kernel, out_shape=(jax.ShapeDtypeStruct((TOK, D), BF...  64 us
    unnamed x8, local copies, waits for them, and re-layouts  5.33 us

profile of v2, /device:TPU:1, one launch (start us, length us, event | category | flops | bytes accessed | tf_op | source)
XLA Modules:
  0.0 69.9 jit_solution(13242332238165160147)
XLA Ops:
  0.6 0.0 copy-start
  0.6 1.6 %copy-done = bf16[1188,896]{1,0:T(8,128)(2,1)S(1)} copy-done((bf16[1188,896]{1,0:T(8,128)(2,1)S(1)}, bf16[1188,896]{1,0:T(8,128)(2,1)}, u32[]{:S(2)}) %copy-start) | copy-done | bytes 2128920
  2.2 0.0 copy-start.1
  2.2 0.8 %copy-done.1 = bf16[128,224]{0,1:T(8,128)(2,1)S(1)} copy-done((bf16[128,224]{0,1:T(8,128)(2,1)S(1)}, bf16[128,224]{0,1:T(8,128)(2,1)}, u32[]{:S(2)}) %copy-start.1) | copy-done | bytes 57368
  3.1 0.0 copy-start.2
  3.1 0.7 copy-done.2
  3.7 64.0 %whole.1 = (bf16[128,3584]{1,0:T(8,128)(2,1)S(1)}, bf16[1188,896]{1,0:T(8,128)(2,1)S(1)}) custom-call(s32[1,128]{1,0:T(1,128)S(1)} %bitcast.3, bf16[1188,896]{1,0:T(8,128)(2,1)S(1)} %copy-done, bf16[224,128]{1,0:T(8,128)(2,1)S(1)} %bitcast.2), custom_call_target="tpu_custom_call" | custom-call | tf_op jit(solution)/shard_map/whole/pallas_call | solution.py:294
  67.7 0.9 %copy.7 = bf16[128,3584]{1,0:T(8,128)(2,1)} copy(bf16[128,3584]{1,0:T(8,128)(2,1)S(1)} %get-tuple-element.4) | data formatting | bytes 1835008
  68.6 1.3 %copy.8 = bf16[1188,896]{1,0:T(8,128)(2,1)} copy(bf16[1188,896]{1,0:T(8,128)(2,1)S(1)} %get-tuple-element.5) | data formatting | bytes 4257792
Async XLA Ops:
  0.6 1.6 %copy-start = (bf16[1188,896]{1,0:T(8,128)(2,1)S(1)}, bf16[1188,896]{1,0:T(8,128)(2,1)}, u32[]{:S(2)}) copy-start(bf16[1188,896]{1,0:T(8,128)(2,1)} %table_hbm.1) | copy-start | bytes 6386692
  2.2 0.8 %copy-start.1 = (bf16[128,224]{0,1:T(8,128)(2,1)S(1)}, bf16[128,224]{0,1:T(8,128)(2,1)}, u32[]{:S(2)}) copy-start(bf16[128,224]{0,1:T(8,128)(2,1)} %param.5) | copy-start | bytes 172036
  3.1 0.7 copy-start.2

commit v3 on v2

--- a/solution.py
+++ b/solution.py
@@ -17,8 +17,9 @@
 FEATS = 224
 BF = jnp.bfloat16
 F32 = jnp.float32
-CUTS = (256, 384, 256)
-STARTS = (0, 256, 640)
+CUTS = (256, 256, 256, 128)
+STARTS = (0, 256, 512, 768)
+N = len(CUTS)
 
 
 def coords():
@@ -39,10 +40,6 @@
     return [(dx, dk) for dx in range(X) for dk in range(YC) if dx or dk]
 
 
-def vmem(n=1):
-    return [pl.BlockSpec(memory_space=pltpu.VMEM)] * n
-
-
 def onehot(condition):
     return jnp.where(condition, F32(1), F32(0)).astype(BF)
 
@@ -74,15 +71,15 @@
 
 
 def whole_kernel(
-    ids_ref, table_hbm, gradt_ref, emb_ref, tg_ref,
-    table, info, mine, piece, got, place_at, gq, order_ref, s_ref, lrow_ref,
-    es0, es1, es2, er0, er1, er2, dr, gs, gr, de0, de1, de2, zr0, zr1, zr2,
-    fs0, fs1, fs2, fr0, fr1, fr2,
-    table_sem, id_send, id_recv, ft_send, ft_recv, zt_send, zt_recv,
-    ab_send, ab_recv, bt_send, bt_recv, z_send, z_recv, f_send, f_recv,
+    ids_hbm, table_hbm, gradt_hbm, emb_hbm, tg_hbm,
+    emb_ref, tg_ref, ids_ref, gradt_ref, table, info, flat, rt_ref, val_ref, mine, piece, got, place_at, gq, order_ref,
+    s_ref, lrow_ref, dr, gs, gr, *rest,
 ):
-    es, er, de, zr = (es0, es1, es2), (er0, er1, er2), (de0, de1, de2), (zr0, zr1, zr2)
-    fs, fr = (fs0, fs1, fs2), (fr0, fr1, fr2)
+    es, er, de, zr, fs, fr, held = (rest[n * N : (n + 1) * N] for n in range(7))
+    (
+        in_sem, id_send, id_recv, ft_send, ft_recv, zt_send, zt_recv, bt_send, bt_recv,
+        ab_send, ab_recv, z_send, z_recv, f_send, f_recv, h_recv, h_send, out_sem, tg_sem,
+    ) = rest[7 * N :]
     zh, k, x, zl = coords()
     z = zh * ZL + zl
     me = x * YC + k
@@ -98,38 +95,26 @@
     for dx, dk in plane:
         to = device(z, (k + dk) % YC, (x + dx) % X)
         pl.semaphore_signal(barrier, inc=1, device_id=to, device_id_type=MESH)
-    table_copy = local(table_hbm, table, table_sem)
-
+    ids_copy = local(ids_hbm, ids_ref, in_sem.at[0])
+    grad_copy = local(gradt_hbm, gradt_ref, in_sem.at[1])
+    table_copy = local(table_hbm, table, in_sem.at[2])
+
+    ids_copy.wait()
     ids = ids_ref[...]
     segment = ((ids.astype(F32) + 0.5) * F32(1.0 / (LINES * PACK))).astype(jnp.int32)
     slot = ids & 7
-    line = (ids - segment * (LINES * PACK)) >> 3
-    bucket = segment * PACK + slot
-    key = (bucket * TOK + lax.broadcasted_iota(jnp.int32, (1, TOK), 1)).astype(F32)
+    key = ((segment * PACK + slot) * TOK + lax.broadcasted_iota(jnp.int32, (1, TOK), 1)).astype(F32)
     keys = jnp.broadcast_to(key, (TOK, TOK))
-    turned = keys.T
-    first = (bucket * TOK).astype(F32)
-    at = jnp.sum(jnp.where(turned < keys, F32(1), F32(0)), axis=0, keepdims=True)
-    begin = jnp.sum(jnp.where(turned < first, F32(1), F32(0)), axis=0, keepdims=True)
+    at = jnp.sum(jnp.where(keys.T < keys, F32(1), F32(0)), axis=0, keepdims=True)
+    mine[:, :TOK] = ids.astype(F32)
+    mine[:, TOK:] = at
     at = at.astype(jnp.int32)
-    second = (at - begin.astype(jnp.int32)) >> 3
     klass, inside = at & 7, at >> 3
-    rows = (
-        line + 1,
-        bucket,
-        klass * 16 + second,
-        klass,
-        inside,
-        ((slot >> 1) * YC + (segment & 7)) * 16 + second,
-        (segment >> 3) * 2 + (slot & 1),
-        slot,
-    )
-    for n, row in enumerate(rows):
-        mine[n : n + 1, :] = row.astype(F32)
     order = jnp.where(
         iota((TOK, TOK), 0) == (klass * 16 + inside).astype(F32), F32(1), F32(0)
     )
     order_ref[...] = order.T.astype(BF)
+    grad_copy.wait()
     sorted_grad = lax.dot_general(
         order.astype(BF), gradt_ref[...], (((1,), (1,)), ((), ())), preferred_element_type=F32
     ).astype(BF)
@@ -177,14 +162,30 @@
             def _():
                 local(gq.at[h], dr.at[zl], zt_recv)
 
+    for g in range(GROUPS):
+        flat[g : g + 1, :] = info[g]
+    ids = flat[:, :TOK]
+    segment = ((ids + 0.5) * F32(1.0 / (LINES * PACK))).astype(jnp.int32)
+    ids = ids.astype(jnp.int32)
+    slot = ids & 7
+    line = (ids - segment * (LINES * PACK)) >> 3
+    at = flat[:, TOK:].astype(jnp.int32)
+    klass, inside = at & 7, at >> 3
+    second = inside & 1
+    zg_row = lax.broadcasted_iota(jnp.int32, (GROUPS, TOK), 0) & 7
+    my_bucket = (zh * YC + k) * PACK + 2 * x + parity
+    code = jnp.where(segment * PACK + slot == my_bucket, klass * 16 + second + 2 * zg_row, -1).astype(F32)
+    line = (line + 1).astype(F32)
+    here = (klass == k) & (segment >> 3 == zh) & (slot & 1 == parity)
+    rt_ref[...] = jnp.where(here, inside + 16 * zg_row, -1).astype(F32)
+    source = ((slot >> 1) * YC + (segment & 7)) * 16 + second
+    val_ref[...] = (source + 2 * zg_row + 1).astype(F32)
+
     sub = iota((TOK, TOK), 0)
-    my_bucket = ((zh * YC + k) * PACK + 2 * x + parity).astype(F32)
     for ox in range(X):
         acc = jnp.zeros((TOK, TOK), F32)
-        for zg in range(ZL):
-            rows = info[ox * ZL + zg]
-            code = jnp.where(rows[1:2] == my_bucket, rows[2:3] + F32(2 * zg), F32(-1))
-            acc = acc + jnp.where(sub == code, rows[0:1], F32(0))
+        for g in range(ox * ZL, (ox + 1) * ZL):
+            acc = acc + jnp.where(sub == code[g : g + 1], line[g : g + 1], F32(0))
         lcol = jnp.sum(acc, axis=1, keepdims=True) - 1
         lrow_ref[:, ox * TOK : (ox + 1) * TOK] = jnp.sum(acc.T, axis=0, keepdims=True) - 1
         s_ref[ox * TOK : (ox + 1) * TOK, :] = onehot(lcol == iota((TOK, LINES), 1))
@@ -207,13 +208,10 @@
         plane_copies(es[c], er[c], ab_send.at[c], ab_recv.at[c])
 
     acc = jnp.zeros((TOK, TOK), F32)
-    my_half = (zh * 2 + parity).astype(F32)
-    my_class = k.astype(F32)
+    own = pl.ds(pl.multiple_of(x * ZL, ZL), ZL)
+    rt, val = rt_ref[own, :], val_ref[own, :]
     for zg in range(ZL):
-        rows = info[x * ZL + zg]
-        here = (rows[3:4] == my_class) & (rows[6:7] == my_half)
-        code = jnp.where(here, rows[4:5] + F32(16 * zg), F32(-1))
-        acc = acc + jnp.where(sub == code, rows[5:6] + F32(2 * zg + 1), F32(0))
+        acc = acc + jnp.where(sub == rt[zg : zg + 1], val[zg : zg + 1], F32(0))
     mcol = jnp.sum(acc, axis=1, keepdims=True) - 1
     mrow = jnp.sum(acc.T, axis=0, keepdims=True) - 1
     merge = onehot(mcol == iota((TOK, 512), 1))
@@ -222,17 +220,29 @@
     def merge_and_send(c):
         settle(er[c], ab_recv.at[c])
         de[c][...] = dot(merge, er[c][...].reshape(512, CUTS[c])).reshape(ZL, 16, CUTS[c])
-        for dz in range(1, Z):
+        opposite = (z + 8) % Z
+        low, high = pl.ds(0, 8), pl.ds(8, 8)
+        remote(de[c].at[opposite % ZL, high], held[c], z_send.at[c], h_recv.at[c], device((z + 12) % Z, k, x))
+        remote(de[c].at[opposite % ZL, low], zr[c].at[z, low], z_send.at[c], z_recv.at[c], device(opposite, k, x))
+        for dz in (9, 7, 10, 6, 11, 5, 12, 4, 13, 3, 14, 2, 15, 1):
             there = (z + dz) % Z
             remote(de[c].at[there % ZL], zr[c].at[z], z_send.at[c], z_recv.at[c], device(there, k, x))
         local(de[c].at[zl], zr[c].at[z], z_recv.at[c])
+
+    def pass_on(c):
+        settle(held[c], h_recv.at[c])
+        behind = device((z + 12) % Z, k, x)
+        remote(held[c], zr[c].at[(z + 4) % Z, pl.ds(8, 8)], h_send.at[c], z_recv.at[c], behind)
 
     merge_and_send(0)
     settle(dr, zt_recv)
     gs[...] = dot(spread, dr[...].reshape(TOK, WIDTH)).reshape(GROUPS, 16, WIDTH)
     merge_and_send(1)
     plane_copies(gs, gr, bt_send, bt_recv)
+    pass_on(0)
     merge_and_send(2)
+    pass_on(1)
+    merge_and_send(3)
 
     def sum_and_send(c):
         settle(zr[c], z_recv.at[c])
@@ -250,10 +260,14 @@
         for quarter in range(4):
             start = quarter * WIDTH + STARTS[c]
             rows = fr[c][:, quarter].reshape(TOK, CUTS[c])
-            emb_ref[:, start : start + CUTS[c]] = dot(order_ref[...], rows)
+            columns = slice(start, start + CUTS[c])
+            emb_ref[:, columns] = dot(order_ref[...], rows)
+            local(emb_ref.at[:, columns], emb_hbm.at[:, columns], out_sem.at[c])
 
     sum_and_send(0)
+    pass_on(2)
     sum_and_send(1)
+    pass_on(3)
     settle(gr, bt_recv)
 
     def scatter(start, rows):
@@ -267,15 +281,21 @@
 
     lax.fori_loop(0, LINES // TOK, scatter_step, 0)
     scatter(LINES // TOK * TOK, LINES % TOK)
+    local(tg_ref, tg_hbm, tg_sem)
     finish(0)
     sum_and_send(2)
     finish(1)
+    sum_and_send(3)
     finish(2)
+    finish(3)
 
     settle(info.at[pl.ds(0, GROUPS - 1)], id_send)
+    settle(tg_ref, tg_sem)
     settle(got.at[pl.ds(0, YC - 1)], ft_send)
     settle(gr.at[pl.ds(0, GROUPS - 1)], bt_send)
-    for c in range(3):
+    for c in range(N):
+        settle(held[c], h_send.at[c])
+        settle(emb_ref.at[:, : 4 * CUTS[c]], out_sem.at[c])
         settle(er[c].at[pl.ds(0, GROUPS - 1)], ab_send.at[c])
         settle(zr[c].at[pl.ds(0, Z - 1)], z_send.at[c])
         settle(fr[c].at[pl.ds(0, YC - 1)], f_send.at[c])
@@ -297,12 +317,19 @@
             jax.ShapeDtypeStruct((TOK, D), BF),
             jax.ShapeDtypeStruct((LINES, WIDTH), BF),
         ),
-        in_specs=[vmem()[0], pl.BlockSpec(memory_space=pl.ANY), vmem()[0]],
-        out_specs=tuple(vmem(2)),
+        in_specs=[pl.BlockSpec(memory_space=pl.ANY)] * 3,
+        out_specs=(pl.BlockSpec(memory_space=pl.ANY),) * 2,
         scratch_shapes=[
+            pltpu.VMEM((TOK, D), BF),
             pltpu.VMEM((LINES, WIDTH), BF),
-            pltpu.VMEM((GROUPS, 8, TOK), F32),
-            pltpu.VMEM((8, TOK), F32),
+            pltpu.VMEM((1, TOK), jnp.int32),
+            pltpu.VMEM((FEATS, TOK), BF),
+            pltpu.VMEM((LINES, WIDTH), BF),
+            pltpu.VMEM((GROUPS, 1, 2 * TOK), F32),
+            pltpu.VMEM((GROUPS, 2 * TOK), F32),
+            pltpu.VMEM((GROUPS, TOK), F32),
+            pltpu.VMEM((GROUPS, TOK), F32),
+            pltpu.VMEM((1, 2 * TOK), F32),
             pltpu.VMEM((YC, 16, FEATS), BF),
             pltpu.VMEM((YC, 16, FEATS), BF),
             pltpu.VMEM((4, FEATS, WIDTH), BF),
@@ -310,20 +337,20 @@
             pltpu.VMEM((TOK, TOK), BF),
             pltpu.VMEM((512, LINES), BF),
             pltpu.VMEM((1, 512), F32),
-            *each(GROUPS, 16),
-            *each(GROUPS, 16),
             pltpu.VMEM((ZL, 16, WIDTH), BF),
             pltpu.VMEM((GROUPS, 16, WIDTH), BF),
             pltpu.VMEM((GROUPS, 16, WIDTH), BF),
+            *each(GROUPS, 16),
+            *each(GROUPS, 16),
             *each(ZL, 16),
             *each(Z, 16),
             *each(4, 16),
             *each(YC, 4, 16),
-            dma, dma, dma, dma, dma, dma((8,)), dma,
-            dma((3,)), dma((3,)), dma, dma, dma((3,)), dma((3,)), dma((3,)), dma((3,)),
+            *each(8),
+            dma((3,)), dma, dma, dma, dma, dma((8,)), dma, dma, dma, *[dma((N,))] * 9, dma,
         ],
         compiler_params=pltpu.CompilerParams(
-            collective_id=0, has_side_effects=True, vmem_limit_bytes=48 * 1024 * 1024
+            collective_id=0, has_side_effects=True, vmem_limit_bytes=60_000_000
         ),
         name="whole",
     )(token_ids.reshape(1, TOK), table, out_grad.T)

time: 70.1 us -> 73.4 us (1.047)
  Pallas kernels: 64 us -> 67.3 us
    pallas_call x1, Pallas kernels: 64 us -> 67.3 us  [body(): pl.pallas_call(whole_kernel, out_shape=(jax.ShapeDtypeStruct((TOK, D), BF...]
    unnamed x8 -> x2, local copies, waits for them, and re-layouts: 5.33 us -> 5.26 us
where the time goes in v3:
time: 73.4 us; the launch traced here: 73.2 us
  Pallas kernels  67.3 us (92%)
  local copies, waits for them, and re-layouts  5.26 us (7%)
    pallas_call x1, Pallas kernels, body(): pl.pallas_call(whole_kernel, out_shape=(jax.ShapeDtypeStruct((TOK, D), BF...  67.3 us
    unnamed x2, local copies, waits for them, and re-layouts  5.26 us

profile of v3, /device:TPU:1, one launch (start us, length us, event | category | flops | bytes accessed | tf_op | source)
XLA Modules:
  0.0 73.2 jit_solution(13221334767958294166)
XLA Ops:
  0.6 67.3 %whole.1 = (bf16[128,3584]{1,0:T(8,128)(2,1)}, bf16[1188,896]{1,0:T(8,128)(2,1)}) custom-call(s32[1,128]{1,0:T(1,128)} %bitcast.3, bf16[1188,896]{1,0:T(8,128)(2,1)} %table_hbm.1, bf16[224,128]{1,0:T(8,128)(2,1)} %bitcast.2), custom_call_target="tpu_custom_call" | custom-call | tf_op jit(solution)/shard_map/whole/pallas_call | solution.py:314
  68.0 2.2 %copy.7 = bf16[128,3584]{1,0:T(8,128)(2,1)} copy(bf16[128,3584]{1,0:T(8,128)(2,1)} %get-tuple-element.4) | data formatting | bytes 1835008
  70.1 3.1 %copy.8 = bf16[1188,896]{1,0:T(8,128)(2,1)} copy(bf16[1188,896]{1,0:T(8,128)(2,1)} %get-tuple-element.5) | data formatting | bytes 4257792

commit v4 on v3

--- a/solution.py
+++ b/solution.py
@@ -17,8 +17,8 @@
 FEATS = 224
 BF = jnp.bfloat16
 F32 = jnp.float32
-CUTS = (256, 256, 256, 128)
-STARTS = (0, 256, 512, 768)
+CUTS = (256, 384, 256)
+STARTS = (0, 256, 640)
 N = len(CUTS)
 
 
@@ -71,15 +71,15 @@
 
 
 def whole_kernel(
-    ids_hbm, table_hbm, gradt_hbm, emb_hbm, tg_hbm,
-    emb_ref, tg_ref, ids_ref, gradt_ref, table, info, flat, rt_ref, val_ref, mine, piece, got, place_at, gq, order_ref,
+    ids_hbm, table_hbm, gradt_hbm, emb_ref, tg_ref,
+    ids_ref, gradt_ref, table, info, flat, rt_ref, val_ref, mine, piece, got, place_at, gq, order_ref,
     s_ref, lrow_ref, dr, gs, gr, *rest,
 ):
-    es, er, de, zr, fs, fr, held = (rest[n * N : (n + 1) * N] for n in range(7))
+    es, er, de, zr, fs, fr = (rest[n * N : (n + 1) * N] for n in range(6))
     (
         in_sem, id_send, id_recv, ft_send, ft_recv, zt_send, zt_recv, bt_send, bt_recv,
-        ab_send, ab_recv, z_send, z_recv, f_send, f_recv, h_recv, h_send, out_sem, tg_sem,
-    ) = rest[7 * N :]
+        ab_send, ab_recv, z_send, z_recv, f_send, f_recv, zt_pass,
+    ) = rest[6 * N :]
     zh, k, x, zl = coords()
     z = zh * ZL + zl
     me = x * YC + k
@@ -138,30 +138,30 @@
         for j in range(4):
             total = total + jnp.dot(got[4 * h + j], place_at[j], preferred_element_type=F32)
         gq[h] = total.astype(BF)
-    settle(info, id_recv)
-
     zt = []
     for h in range(2):
-        for m in range(4):
-            there = 2 * zh + h + 4 * m
-            copy = pltpu.make_async_remote_copy(
-                src_ref=gq.at[h],
-                dst_ref=dr.at[zl],
-                send_sem=zt_send.at[h * 4 + m],
-                recv_sem=zt_recv,
-                device_id=device(there, k, x),
-                device_id_type=MESH,
-            )
-            zt.append((there, copy))
-
-            @pl.when(there != z)
-            def _():
-                copy.start()
-
-            @pl.when(there == z)
-            def _():
-                local(gq.at[h], dr.at[zl], zt_recv)
-
+        ahead = (2 * zh + h + 4 - zl % 4) % 4
+        up = pltpu.make_async_remote_copy(
+            src_ref=gq.at[h],
+            dst_ref=dr.at[zl],
+            send_sem=zt_send.at[h],
+            recv_sem=zt_recv.at[zl],
+            device_id=device((z + ahead) % Z, k, x),
+            device_id_type=MESH,
+        )
+        zt.append((ahead, up))
+
+        @pl.when(ahead != 0)
+        def _():
+            up.start()
+
+        @pl.when(ahead == 0)
+        def _():
+            local(gq.at[h], dr.at[zl], zt_recv.at[zl])
+
+        remote(gq.at[h], dr.at[zl], zt_send.at[2 + h], zt_recv.at[zl], device((z + ahead + 12) % Z, k, x))
+
+    settle(info, id_recv)
     for g in range(GROUPS):
         flat[g : g + 1, :] = info[g]
     ids = flat[:, :TOK]
@@ -197,6 +197,20 @@
             remote(src.at[ox * YC + ok], dst.at[me], send, recv, device(z, ok, ox))
         local(src.at[me], dst.at[me], recv)
 
+    past = [(z + Z - zl % 4 // 2 * ZL - zg) % Z for zg in range(ZL)]
+
+    def pass_gradients():
+        for zg, d in enumerate(past):
+            @pl.when(d < 4)
+            def _():
+                settle(dr.at[zg], zt_recv.at[zg])
+                remote(dr.at[zg], dr.at[zg], zt_pass.at[zg], zt_recv.at[zg], device((z + 4) % Z, k, x))
+
+            @pl.when(d >= 12)
+            def _():
+                settle(dr.at[zg], zt_recv.at[zg])
+                remote(dr.at[zg], dr.at[zg], zt_pass.at[zg], zt_recv.at[zg], device((z + 12) % Z, k, x))
+
     for c, (start, width) in enumerate(zip(STARTS, CUTS)):
         def pick_rows(i, carry):
             rows = pl.ds(pl.multiple_of(i * TOK, TOK), TOK)
@@ -206,6 +220,8 @@
 
         lax.fori_loop(0, 4, pick_rows, 0)
         plane_copies(es[c], er[c], ab_send.at[c], ab_recv.at[c])
+        if c == 0:
+            pass_gradients()
 
     acc = jnp.zeros((TOK, TOK), F32)
     own = pl.ds(pl.multiple_of(x * ZL, ZL), ZL)
@@ -221,28 +237,22 @@
         settle(er[c], ab_recv.at[c])
         de[c][...] = dot(merge, er[c][...].reshape(512, CUTS[c])).reshape(ZL, 16, CUTS[c])
         opposite = (z + 8) % Z
-        low, high = pl.ds(0, 8), pl.ds(8, 8)
-        remote(de[c].at[opposite % ZL, high], held[c], z_send.at[c], h_recv.at[c], device((z + 12) % Z, k, x))
-        remote(de[c].at[opposite % ZL, low], zr[c].at[z, low], z_send.at[c], z_recv.at[c], device(opposite, k, x))
+        remote(de[c].at[opposite % ZL], zr[c].at[z], z_send.at[c], z_recv.at[c], device(opposite, k, x))
         for dz in (9, 7, 10, 6, 11, 5, 12, 4, 13, 3, 14, 2, 15, 1):
             there = (z + dz) % Z
             remote(de[c].at[there % ZL], zr[c].at[z], z_send.at[c], z_recv.at[c], device(there, k, x))
         local(de[c].at[zl], zr[c].at[z], z_recv.at[c])
 
-    def pass_on(c):
-        settle(held[c], h_recv.at[c])
-        behind = device((z + 12) % Z, k, x)
-        remote(held[c], zr[c].at[(z + 4) % Z, pl.ds(8, 8)], h_send.at[c], z_recv.at[c], behind)
-
     merge_and_send(0)
-    settle(dr, zt_recv)
+    for zg, d in enumerate(past):
+        @pl.when((d >= 4) & (d < 12))
+        def _():
+            settle(dr.at[zg], zt_recv.at[zg])
     gs[...] = dot(spread, dr[...].reshape(TOK, WIDTH)).reshape(GROUPS, 16, WIDTH)
     merge_and_send(1)
     plane_copies(gs, gr, bt_send, bt_recv)
-    pass_on(0)
-    merge_and_send(2)
-    pass_on(1)
-    merge_and_send(3)
+    for c in range(2, N):
+        merge_and_send(c)
 
     def sum_and_send(c):
         settle(zr[c], z_recv.at[c])
@@ -262,13 +272,6 @@
             rows = fr[c][:, quarter].reshape(TOK, CUTS[c])
             columns = slice(start, start + CUTS[c])
             emb_ref[:, columns] = dot(order_ref[...], rows)
-            local(emb_ref.at[:, columns], emb_hbm.at[:, columns], out_sem.at[c])
-
-    sum_and_send(0)
-    pass_on(2)
-    sum_and_send(1)
-    pass_on(3)
-    settle(gr, bt_recv)
 
     def scatter(start, rows):
         line = (start + lax.broadcasted_iota(jnp.int32, (rows, 512), 0)).astype(F32)
@@ -279,30 +282,35 @@
         scatter(pl.multiple_of(i * TOK, TOK), TOK)
         return carry
 
+    sum_and_send(0)
+    sum_and_send(1)
+    for c in range(2, N):
+        finish(c - 2)
+        sum_and_send(c)
+    settle(gr, bt_recv)
     lax.fori_loop(0, LINES // TOK, scatter_step, 0)
     scatter(LINES // TOK * TOK, LINES % TOK)
-    local(tg_ref, tg_hbm, tg_sem)
-    finish(0)
-    sum_and_send(2)
-    finish(1)
-    sum_and_send(3)
-    finish(2)
-    finish(3)
+    finish(N - 2)
+    finish(N - 1)
 
     settle(info.at[pl.ds(0, GROUPS - 1)], id_send)
-    settle(tg_ref, tg_sem)
     settle(got.at[pl.ds(0, YC - 1)], ft_send)
     settle(gr.at[pl.ds(0, GROUPS - 1)], bt_send)
     for c in range(N):
-        settle(held[c], h_send.at[c])
-        settle(emb_ref.at[:, : 4 * CUTS[c]], out_sem.at[c])
         settle(er[c].at[pl.ds(0, GROUPS - 1)], ab_send.at[c])
         settle(zr[c].at[pl.ds(0, Z - 1)], z_send.at[c])
         settle(fr[c].at[pl.ds(0, YC - 1)], f_send.at[c])
-    for there, copy in zt:
-        @pl.when(there != z)
-        def _():
-            copy.wait_send()
+    for h, (ahead, up) in enumerate(zt):
+        settle(gq.at[h], zt_send.at[2 + h])
+
+        @pl.when(ahead != 0)
+        def _():
+            up.wait_send()
+
+    for zg, d in enumerate(past):
+        @pl.when((d < 4) | (d >= 12))
+        def _():
+            settle(dr.at[zg], zt_pass.at[zg])
 
 
 def body(token_ids, table, out_grad):
@@ -318,10 +326,8 @@
             jax.ShapeDtypeStruct((LINES, WIDTH), BF),
         ),
         in_specs=[pl.BlockSpec(memory_space=pl.ANY)] * 3,
-        out_specs=(pl.BlockSpec(memory_space=pl.ANY),) * 2,
+        out_specs=(pl.BlockSpec(memory_space=pltpu.VMEM),) * 2,
         scratch_shapes=[
-            pltpu.VMEM((TOK, D), BF),
-            pltpu.VMEM((LINES, WIDTH), BF),
             pltpu.VMEM((1, TOK), jnp.int32),
             pltpu.VMEM((FEATS, TOK), BF),
             pltpu.VMEM((LINES, WIDTH), BF),
@@ -346,11 +352,10 @@
             *each(Z, 16),
             *each(4, 16),
             *each(YC, 4, 16),
-            *each(8),
-            dma((3,)), dma, dma, dma, dma, dma((8,)), dma, dma, dma, *[dma((N,))] * 9, dma,
+            dma((3,)), dma, dma, dma, dma, dma((4,)), dma((8,)), dma, dma, *[dma((N,))] * 6, dma((8,)),
         ],
         compiler_params=pltpu.CompilerParams(
-            collective_id=0, has_side_effects=True, vmem_limit_bytes=60_000_000
+            collective_id=0, has_side_effects=True, vmem_limit_bytes=52_500_000
         ),
         name="whole",
     )(token_ids.reshape(1, TOK), table, out_grad.T)

time: 73.4 us -> 65.7 us (0.90)
  Pallas kernels: 67.3 us -> 61.2 us
  local copies, waits for them, and re-layouts: 5.26 us -> 3.72 us
    pallas_call x1, Pallas kernels: 67.3 us -> 61.2 us  [body(): pl.pallas_call(whole_kernel, out_shape=(jax.ShapeDtypeStruct((TOK, D), BF...]
    unnamed x2 -> x6, local copies, waits for them, and re-layouts: 5.26 us -> 3.72 us
where the time goes in v4:
time: 65.7 us; the launch traced here: 65.6 us
  Pallas kernels  61.2 us (93%)
  local copies, waits for them, and re-layouts  3.72 us (6%)
    pallas_call x1, Pallas kernels, body(): pl.pallas_call(whole_kernel, out_shape=(jax.ShapeDtypeStruct((TOK, D), BF...  61.2 us
    unnamed x6, local copies, waits for them, and re-layouts  3.72 us

profile of v4, /device:TPU:1, one launch (start us, length us, event | category | flops | bytes accessed | tf_op | source)
XLA Modules:
  0.0 65.6 jit_solution(14679405954359110033)
XLA Ops:
  0.6 0.0 copy-start
  0.6 0.8 %copy-done = bf16[128,224]{0,1:T(8,128)(2,1)S(1)} copy-done((bf16[128,224]{0,1:T(8,128)(2,1)S(1)}, bf16[128,224]{0,1:T(8,128)(2,1)}, u32[]{:S(2)}) %copy-start) | copy-done | bytes 57368
  1.4 0.0 copy-start.1
  1.5 0.7 copy-done.1
  2.1 61.2 %whole.1 = (bf16[128,3584]{1,0:T(8,128)(2,1)S(1)}, bf16[1188,896]{1,0:T(8,128)(2,1)S(1)}) custom-call(s32[1,128]{1,0:T(1,128)S(1)} %bitcast.3, bf16[1188,896]{1,0:T(8,128)(2,1)} %table_hbm.1, bf16[224,128]{1,0:T(8,128)(2,1)S(1)} %bitcast.2), custom_call_target="tpu_custom_call" | custom-call | tf_op jit(solution)/shard_map/whole/pallas_call | solution.py:322
  63.3 0.9 %copy.7 = bf16[128,3584]{1,0:T(8,128)(2,1)} copy(bf16[128,3584]{1,0:T(8,128)(2,1)S(1)} %get-tuple-element.4) | data formatting | bytes 1835008
  64.2 1.3 %copy.8 = bf16[1188,896]{1,0:T(8,128)(2,1)} copy(bf16[1188,896]{1,0:T(8,128)(2,1)S(1)} %get-tuple-element.5) | data formatting | bytes 4257792
Async XLA Ops:
  0.6 0.8 %copy-start = (bf16[128,224]{0,1:T(8,128)(2,1)S(1)}, bf16[128,224]{0,1:T(8,128)(2,1)}, u32[]{:S(2)}) copy-start(bf16[128,224]{0,1:T(8,128)(2,1)} %param.5) | copy-start | bytes 172036
  1.4 0.7 copy-start.1

commit v5 on v4

--- a/solution.py
+++ b/solution.py
@@ -72,7 +72,7 @@
 
 def whole_kernel(
     ids_hbm, table_hbm, gradt_hbm, emb_ref, tg_ref,
-    ids_ref, gradt_ref, table, info, flat, rt_ref, val_ref, mine, piece, got, place_at, gq, order_ref,
+    ids_ref, gradt_ref, table, info, flat, code_ref, line_ref, found_ref, rt_ref, val_ref, mine, piece, got, gq, order_ref,
     s_ref, lrow_ref, dr, gs, gr, *rest,
 ):
     es, er, de, zr, fs, fr = (rest[n * N : (n + 1) * N] for n in range(6))
@@ -119,9 +119,6 @@
         order.astype(BF), gradt_ref[...], (((1,), (1,)), ((), ())), preferred_element_type=F32
     ).astype(BF)
     piece[...] = sorted_grad.reshape(YC, 16, FEATS)
-    for j in range(4):
-        place_at[j] = onehot(iota((FEATS, WIDTH), 0) + F32(FEATS * j) == iota((FEATS, WIDTH), 1))
-
     pl.semaphore_wait(barrier, len(near) + len(plane))
 
     for dx, dz in [(dx, dz) for dx in range(X) for dz in range(-3, 5) if dx or dz]:
@@ -134,10 +131,8 @@
 
     settle(got, ft_recv)
     for h in range(2):
-        total = jnp.zeros((16, WIDTH), F32)
-        for j in range(4):
-            total = total + jnp.dot(got[4 * h + j], place_at[j], preferred_element_type=F32)
-        gq[h] = total.astype(BF)
+        quarters = [got[4 * h + j].astype(F32) for j in range(4)]
+        gq[h] = jnp.concatenate(quarters, axis=1).astype(BF)
     zt = []
     for h in range(2):
         ahead = (2 * zh + h + 4 - zl % 4) % 4
@@ -181,15 +176,29 @@
     source = ((slot >> 1) * YC + (segment & 7)) * 16 + second
     val_ref[...] = (source + 2 * zg_row + 1).astype(F32)
 
+    code_ref[...] = code
+    line_ref[...] = line
+
     sub = iota((TOK, TOK), 0)
-    for ox in range(X):
+    table_copy.wait()
+    for dx in range(X):
+        ox = (x + dx) % X
+        groups = pl.ds(pl.multiple_of(ox * ZL, ZL), ZL)
+        codes, lines = code_ref[groups, :], line_ref[groups, :]
         acc = jnp.zeros((TOK, TOK), F32)
-        for g in range(ox * ZL, (ox + 1) * ZL):
-            acc = acc + jnp.where(sub == code[g : g + 1], line[g : g + 1], F32(0))
+        for zg in range(ZL):
+            acc = acc + jnp.where(sub == codes[zg : zg + 1], lines[zg : zg + 1], F32(0))
+        found_ref[ox] = acc
         lcol = jnp.sum(acc, axis=1, keepdims=True) - 1
-        lrow_ref[:, ox * TOK : (ox + 1) * TOK] = jnp.sum(acc.T, axis=0, keepdims=True) - 1
-        s_ref[ox * TOK : (ox + 1) * TOK, :] = onehot(lcol == iota((TOK, LINES), 1))
-    table_copy.wait()
+        pick = onehot(lcol == iota((TOK, LINES), 1))
+        s_ref[pl.ds(pl.multiple_of(ox * TOK, TOK), TOK), :] = pick
+        es[0][pl.ds(ox * YC, YC)] = dot(pick, table[:, : CUTS[0]]).reshape(YC, 16, CUTS[0])
+        for dk in range(YC):
+            ok = (k + dk) % YC
+            if dx or dk:
+                remote(es[0].at[ox * YC + ok], er[0].at[me], ab_send.at[0], ab_recv.at[0], device(z, ok, ox))
+            else:
+                local(es[0].at[me], er[0].at[me], ab_recv.at[0])
 
     def plane_copies(src, dst, send, recv):
         for dx, dk in plane:
@@ -211,17 +220,16 @@
                 settle(dr.at[zg], zt_recv.at[zg])
                 remote(dr.at[zg], dr.at[zg], zt_pass.at[zg], zt_recv.at[zg], device((z + 12) % Z, k, x))
 
-    for c, (start, width) in enumerate(zip(STARTS, CUTS)):
+    pass_gradients()
+    for c in range(1, N):
         def pick_rows(i, carry):
             rows = pl.ds(pl.multiple_of(i * TOK, TOK), TOK)
-            picked = dot(s_ref[rows, :], table[:, start : start + width])
-            es[c][pl.ds(i * 8, 8)] = picked.reshape(8, 16, width)
+            picked = dot(s_ref[rows, :], table[:, STARTS[c] : STARTS[c] + CUTS[c]])
+            es[c][pl.ds(i * 8, 8)] = picked.reshape(8, 16, CUTS[c])
             return carry
 
         lax.fori_loop(0, 4, pick_rows, 0)
         plane_copies(es[c], er[c], ab_send.at[c], ab_recv.at[c])
-        if c == 0:
-            pass_gradients()
 
     acc = jnp.zeros((TOK, TOK), F32)
     own = pl.ds(pl.multiple_of(x * ZL, ZL), ZL)
@@ -287,6 +295,8 @@
     for c in range(2, N):
         finish(c - 2)
         sum_and_send(c)
+    for ox in range(X):
+        lrow_ref[:, ox * TOK : (ox + 1) * TOK] = jnp.sum(found_ref[ox].T, axis=0, keepdims=True) - 1
     settle(gr, bt_recv)
     lax.fori_loop(0, LINES // TOK, scatter_step, 0)
     scatter(LINES // TOK * TOK, LINES % TOK)
@@ -335,10 +345,12 @@
             pltpu.VMEM((GROUPS, 2 * TOK), F32),
             pltpu.VMEM((GROUPS, TOK), F32),
             pltpu.VMEM((GROUPS, TOK), F32),
+            pltpu.VMEM((X, TOK, TOK), F32),
+            pltpu.VMEM((GROUPS, TOK), F32),
+            pltpu.VMEM((GROUPS, TOK), F32),
             pltpu.VMEM((1, 2 * TOK), F32),
             pltpu.VMEM((YC, 16, FEATS), BF),
             pltpu.VMEM((YC, 16, FEATS), BF),
-            pltpu.VMEM((4, FEATS, WIDTH), BF),
             pltpu.VMEM((2, 16, WIDTH), BF),
             pltpu.VMEM((TOK, TOK), BF),
             pltpu.VMEM((512, LINES), BF),

time: 65.7 us -> 64.8 us (0.986)
  Pallas kernels: 61.2 us -> 60.3 us
    pallas_call x1, Pallas kernels: 61.2 us -> 60.3 us  [body(): pl.pallas_call(whole_kernel, out_shape=(jax.ShapeDtypeStruct((TOK, D), BF...]
where the time goes in v5:
time: 64.8 us; the launch traced here: 64.6 us
  Pallas kernels  60.3 us (93%)
  local copies, waits for them, and re-layouts  3.72 us (6%)
  between operations  0.65 us (1%)
    pallas_call x1, Pallas kernels, body(): pl.pallas_call(whole_kernel, out_shape=(jax.ShapeDtypeStruct((TOK, D), BF...  60.3 us
    unnamed x6, local copies, waits for them, and re-layouts  3.72 us

profile of v5, /device:TPU:1, one launch (start us, length us, event | category | flops | bytes accessed | tf_op | source)
XLA Modules:
  0.0 64.6 jit_solution(6083356922930360113)
XLA Ops:
  0.6 0.0 copy-start
  0.6 0.8 %copy-done = bf16[128,224]{0,1:T(8,128)(2,1)S(1)} copy-done((bf16[128,224]{0,1:T(8,128)(2,1)S(1)}, bf16[128,224]{0,1:T(8,128)(2,1)}, u32[]{:S(2)}) %copy-start) | copy-done | bytes 57368
  1.4 0.0 copy-start.1
  1.5 0.7 %copy-done.1 = s32[128]{0:T(128)S(1)} copy-done((s32[128]{0:T(128)S(1)}, s32[128]{0:T(128)}, u32[]{:S(2)}) %copy-start.1) | copy-done | bytes 536
  2.1 60.3 %whole.1 = (bf16[128,3584]{1,0:T(8,128)(2,1)S(1)}, bf16[1188,896]{1,0:T(8,128)(2,1)S(1)}) custom-call(s32[1,128]{1,0:T(1,128)S(1)} %bitcast.3, bf16[1188,896]{1,0:T(8,128)(2,1)} %table_hbm.1, bf16[224,128]{1,0:T(8,128)(2,1)S(1)} %bitcast.2), custom_call_target="tpu_custom_call" | custom-call | tf_op jit(solution)/shard_map/whole/pallas_call | solution.py:332
  62.4 0.9 %copy.7 = bf16[128,3584]{1,0:T(8,128)(2,1)} copy(bf16[128,3584]{1,0:T(8,128)(2,1)S(1)} %get-tuple-element.4) | data formatting | bytes 1835008
  63.3 1.3 %copy.8 = bf16[1188,896]{1,0:T(8,128)(2,1)} copy(bf16[1188,896]{1,0:T(8,128)(2,1)S(1)} %get-tuple-element.5) | data formatting | bytes 4257792
Async XLA Ops:
  0.6 0.8 %copy-start = (bf16[128,224]{0,1:T(8,128)(2,1)S(1)}, bf16[128,224]{0,1:T(8,128)(2,1)}, u32[]{:S(2)}) copy-start(bf16[128,224]{0,1:T(8,128)(2,1)} %param.5) | copy-start | bytes 172036
  1.4 0.7 %copy-start.1 = (s32[128]{0:T(128)S(1)}, s32[128]{0:T(128)}, u32[]{:S(2)}) copy-start(s32[128]{0:T(128)} %param.3) | copy-start | bytes 1540
